TPU v7x, 256 devices: a whole 4x4x8 slice. The times are simulated.
256 devices in a mesh: gx: 16 (over z, core), gy: 8 (over y, x_lo), ma: 2 (over x_hi).
Axes of the slice: x: 4 (x_hi: 2, x_lo: 2; x = x_hi * 2 + x_lo), y: 4, z: 8, core: 2. Of those that a mesh axis runs over, the one named last changes fastest.
Arguments:
- archive: bfloat16 [512, 32, 32, 1024], P('ma', 'gx', None, 'gy')
- obs_index: int32 [65536], P(('gx', 'gy', 'ma')), may hold values from 0 to 4095
- obs_value: float32 [65536], P(('gx', 'gy', 'ma')), may hold values from -6 to 6
- obs_error: float32 [65536], P(('gx', 'gy', 'ma')), may hold values from 0.1 to 1
Outputs:
- increment: float32 [32, 32, 1024], P('gx', 'ma', 'gy')
- weights: float32 [65536], P(('gx', 'gy', 'ma'))
All inputs are finite; a program needn't handle non-finite values.
Results may differ from a plain program's by a relative error of at most 0.0018.
Values may be sent and summed in bfloat16 or wider, within the bound.
A program may use at most 64 MiB of HBM per device.

v0:
```python
import functools
import math

import jax
import jax.numpy as jnp
from jax import lax
from jax.experimental import pallas as pl
from jax.experimental.pallas import tpu as pltpu
from jax.sharding import PartitionSpec as P

M = 512
TAPER_X = 4
TAPER_Y = 8
F32 = jnp.float32
BF16 = jnp.bfloat16
MESH = pl.DeviceIdType.MESH

LOADS = 8
CHUNKS = 4
NEAR = (-3, -2, -1, 1, 2, 3)
FAR = 4


def row_weight(distance):
    r = abs(distance) / TAPER_X
    if r <= 1.0:
        return (((-0.25 * r + 0.5) * r + 0.625) * r - 5.0 / 3.0) * r * r + 1.0
    if r < 2.0:
        return (
            ((((r / 12.0 - 0.5) * r + 0.625) * r + 5.0 / 3.0) * r - 5.0) * r
            + 4.0
            - 2.0 / (3.0 * r)
        )
    return 0.0


def taper_weight(distance, half_width):
    ratio = jnp.abs(distance) / half_width
    safe = jnp.maximum(ratio, 1.0)
    inner = (((-0.25 * ratio + 0.5) * ratio + 0.625) * ratio - 5.0 / 3.0) * ratio * ratio + 1.0
    outer = (
        ((((ratio / 12.0 - 0.5) * ratio + 0.625) * ratio + 5.0 / 3.0) * ratio - 5.0) * ratio
        + 4.0
        - 2.0 / (3.0 * safe)
    )
    return jnp.where(ratio <= 1.0, inner, jnp.where(ratio < 2.0, outer, 0.0))


def in_three(x):
    first = x.astype(BF16)
    rest = x - first.astype(F32)
    second = rest.astype(BF16)
    third = (rest - second.astype(F32)).astype(BF16)
    return jnp.concatenate([first, second, third], axis=0)


def sum_of_three(y, rows):
    return (y[2 * rows :] + y[rows : 2 * rows]) + y[:rows]


def kernel(
    n_gx,
    n_gy,
    archive_hbm,
    idx_ref,
    val_ref,
    err_ref,
    inc_ref,
    w_ref,
    arch,
    meta,
    sums,
    part,
    s_ref,
    t_ref,
    near_out,
    near_in,
    far_in,
    f_ref,
    halo_out,
    halo_in,
    wcol,
    pmine,
    ptheirs,
    gsum,
    red1,
    red2,
    load_sem,
    meta_sem,
    sums_sem,
    near_send,
    near_recv,
    far_send,
    far_recv,
    halo_send,
    halo_recv,
    p_sem,
    g_sem,
    red_send,
    red_recv,
):
    members = arch.shape[0]
    levels = arch.shape[2]
    half = levels // 2
    cols = arch.shape[3]
    piece = members // CHUNKS
    gx = lax.axis_index("gx")
    gy = lax.axis_index("gy")
    ma = lax.axis_index("ma")
    other = 1 - ma
    plane = gy * 2 + ma
    n_plane = n_gy * 2

    def row_block(k):
        return {"gx": lax.rem(gx + (k + n_gx), n_gx)}

    def col_block(k):
        return {"gy": lax.rem(gy + (k + n_gy), n_gy)}

    def plane_device(k):
        at = lax.rem(plane + k, n_plane)
        return {"gy": at // 2, "ma": lax.rem(at, 2)}

    load = members // LOADS
    loads = []
    for k in range(LOADS):
        copy = pltpu.make_async_copy(
            archive_hbm.at[pl.ds(k * load, load)], arch.at[pl.ds(k * load, load)], load_sem.at[k]
        )
        copy.start()
        loads.append(copy)

    barrier = pltpu.get_barrier_semaphore()
    for k in range(1, n_gx):
        pl.semaphore_signal(barrier, inc=1, device_id=row_block(k), device_id_type=MESH)
    for k in range(1, n_plane):
        pl.semaphore_signal(barrier, inc=1, device_id=plane_device(k), device_id_type=MESH)

    meta[ma, 0:2, :] = idx_ref[...].astype(F32)
    meta[ma, 2:4, :] = val_ref[...]
    meta[ma, 4:6, :] = err_ref[...]
    meta[ma, 6:8, :] = jnp.zeros((2, cols), F32)

    total = tuple(jnp.zeros((levels, cols), F32) for _ in range(2))
    for k in range(LOADS):
        loads[k].wait()

        def add(m, carry):
            return tuple(carry[x] + arch[m, x].astype(F32) for x in range(2))

        total = lax.fori_loop(k * load, (k + 1) * load, add, total, unroll=8)
    for x in range(2):
        sums[ma, x * levels : (x + 1) * levels, :] = total[x]

    pl.semaphore_wait(barrier, n_gx - 1 + n_plane - 1)

    def to_partner(ref, sem):
        return pltpu.make_async_remote_copy(
            src_ref=ref.at[ma],
            dst_ref=ref.at[ma],
            send_sem=sem.at[0],
            recv_sem=sem.at[1],
            device_id={"ma": other},
            device_id_type=MESH,
        )

    meta_copy = to_partner(meta, meta_sem)
    meta_copy.start()
    sums_copy = to_partner(sums, sums_sem)
    sums_copy.start()

    source = lax.broadcasted_iota(jnp.int32, (cols, cols), 0)
    target = lax.broadcasted_iota(jnp.int32, (cols, cols), 1)
    for k in range(3):
        weight = taper_weight((source - target + (k - 1) * cols).astype(F32), float(TAPER_Y))
        if k == 0:
            weight = jnp.where(gy > 0, weight, 0.0)
        if k == 2:
            weight = jnp.where(gy < n_gy - 1, weight, 0.0)
        high = weight.astype(BF16)
        low = (weight - high.astype(F32)).astype(BF16)
        wcol[k * 2 * cols : (k * 2 + 1) * cols, :] = high
        wcol[(k * 2 + 1) * cols : (k * 2 + 2) * cols, :] = low

    meta_copy.wait()

    def in_a_row(first):
        rows = [meta[h, first + i : first + i + 1, :] for h in range(2) for i in range(2)]
        return jnp.concatenate(rows, axis=1)

    index = in_a_row(0).astype(jnp.int32)
    target_value = in_a_row(2)
    noise = in_a_row(4)
    n_obs = index.shape[1]
    owner = lax.broadcasted_iota(jnp.int32, (1, n_obs), 1) // (n_obs // 2)
    obs_line = (index >> 11) * levels + owner * half + ((index >> 7) & (half - 1))
    obs_col = index & (cols - 1)
    line_hot = (
        lax.broadcasted_iota(jnp.int32, (2 * levels, n_obs), 0) == obs_line
    ).astype(F32)
    col_hot = (
        (lax.broadcasted_iota(jnp.int32, (cols, n_obs), 0) == obs_col).astype(F32).astype(BF16)
    )

    def gather(grid):
        rows = 2 * levels
        spread = jnp.dot(in_three(grid), col_hot, preferred_element_type=F32)
        return jnp.sum(sum_of_three(spread, rows) * line_hot, axis=0, keepdims=True)

    def scatter(vector):
        rows = 2 * levels
        spread = lax.dot_general(
            in_three(line_hot * vector),
            col_hot,
            (((1,), (1,)), ((), ())),
            preferred_element_type=F32,
        )
        return sum_of_three(spread, rows)

    sums_copy.wait()
    average = (sums[0] + sums[1]) * (1.0 / M)
    innovation = target_value - gather(average)
    scale = 1.0 / math.sqrt(M - 1.0)

    def send_sources(phase, q):
        copies = []
        for n, k in enumerate(NEAR):
            copies.append(
                pltpu.make_async_remote_copy(
                    src_ref=near_out.at[phase, q],
                    dst_ref=near_in.at[phase, q, len(NEAR) - 1 - n],
                    send_sem=near_send.at[phase, q, n],
                    recv_sem=near_recv.at[phase, q, len(NEAR) - 1 - n],
                    device_id=row_block(k),
                    device_id_type=MESH,
                )
            )
        for side in range(2):
            copies.append(
                pltpu.make_async_remote_copy(
                    src_ref=near_out.at[phase, q, 1 - side],
                    dst_ref=far_in.at[phase, q, side],
                    send_sem=far_send.at[phase, q, side],
                    recv_sem=far_recv.at[phase, q, side],
                    device_id=row_block(FAR if side == 0 else -FAR),
                    device_id_type=MESH,
                )
            )
        for copy in copies:
            copy.start()
        return copies

    def form_sources(phase, q, grid):
        value = [grid[x * levels : (x + 1) * levels] for x in range(2)]
        mean = [average[x * levels : (x + 1) * levels] for x in range(2)]

        def one(i, carry):
            m = q * piece + i
            for x in range(2):
                if phase == 0:
                    anomaly = ((arch[m, x].astype(F32) - mean[x]) * scale).astype(BF16)
                    arch[m, x] = anomaly
                else:
                    anomaly = arch[m, x]
                product = anomaly.astype(F32) * value[x]
                part[x, pl.ds(pl.multiple_of(i * 8, 8), 8), :] = (
                    product[0:8] + product[8:16]
                ) + (product[16:24] + product[24:32])
            return carry

        lax.fori_loop(0, piece, one, 0, unroll=4)
        for x in range(2):
            for g in range(piece // 8):
                rows = [part[x, pl.ds(g * 64 + k, 8, stride=8), :] for k in range(8)]
                s_ref[phase, x, q * piece + g * 8 : q * piece + g * 8 + 8, :] = (
                    (rows[0] + rows[1]) + (rows[2] + rows[3])
                ) + ((rows[4] + rows[5]) + (rows[6] + rows[7]))
            near_out[phase, q, x] = s_ref[phase, x, q * piece : (q + 1) * piece, :].astype(BF16)

    def filter_rows(phase, q, copies):
        for copy in copies:
            copy.wait_recv()
        for i in range(2):
            out = None
            for r in range(2):
                terms = [(row_weight(r - i), s_ref[phase, r, q * piece : (q + 1) * piece, :])]
                for n, k in enumerate(NEAR):
                    terms.append((row_weight(2 * k + r - i), near_in[phase, q, n, r].astype(F32)))
                for weight, row in terms:
                    if weight:
                        out = row * weight if out is None else out + row * weight
            if i == 0:
                out = out + far_in[phase, q, 0].astype(F32) * row_weight(-2 * FAR + 1)
            else:
                out = out + far_in[phase, q, 1].astype(F32) * row_weight(2 * FAR - 1)
            f_ref[phase, q, i] = out
            halo_out[phase, q, i] = out.astype(BF16)
        sends = []
        for side in range(2):
            copy = pltpu.make_async_remote_copy(
                src_ref=halo_out.at[phase, q],
                dst_ref=halo_in.at[phase, q, side],
                send_sem=halo_send.at[phase, q, side],
                recv_sem=halo_recv.at[phase, q, side],
                device_id=col_block(1 if side == 0 else -1),
                device_id_type=MESH,
            )
            copy.start()
            sends.append(copy)
        return sends

    def filter_cols(phase, q, copies):
        for copy in copies:
            copy.wait_recv()
        rows = 2 * piece
        field = f_ref[phase, q].reshape(rows, cols)
        high = field.astype(BF16)
        low = (field - high.astype(F32)).astype(BF16)
        left = halo_in[phase, q, 0].reshape(rows, cols)
        right = halo_in[phase, q, 1].reshape(rows, cols)
        result = jnp.dot(
            jnp.concatenate([left, left, high, high, right, right], axis=1),
            wcol[...],
            preferred_element_type=F32,
        ) + jnp.dot(low, wcol[2 * cols : 3 * cols, :], preferred_element_type=F32)
        for x in range(2):
            t_ref[phase, x, q * piece : (q + 1) * piece, :] = result[
                x * piece : (x + 1) * piece
            ]

    def member_sum(phase, q, carry):
        def one(i, carry):
            m = q * piece + i
            return tuple(
                carry[x] + arch[m, x].astype(F32) * t_ref[phase, x, pl.ds(m, 1), :]
                for x in range(2)
            )

        return lax.fori_loop(0, piece, one, carry, unroll=4)

    def spread(phase, grid, before_last):
        sent = []
        for q in range(CHUNKS):
            form_sources(phase, q, grid)
            sent.append(send_sources(phase, q))
        halos = []
        carry = tuple(jnp.zeros((levels, cols), F32) for _ in range(2))
        for q in range(CHUNKS):
            halos.append(filter_rows(phase, q, sent[q]))
            if q == 0:
                before_last()
            else:
                filter_cols(phase, q - 1, halos[q - 1])
                carry = member_sum(phase, q - 1, carry)
        filter_cols(phase, CHUNKS - 1, halos[CHUNKS - 1])
        carry = member_sum(phase, CHUNKS - 1, carry)
        for x in range(2):
            for h in range(2):
                pmine[phase, h, x] = carry[x][h * half : (h + 1) * half]
        copy = pltpu.make_async_remote_copy(
            src_ref=pmine.at[phase, other],
            dst_ref=ptheirs.at[phase],
            send_sem=p_sem.at[phase, 0],
            recv_sem=p_sem.at[phase, 1],
            device_id={"ma": other},
            device_id_type=MESH,
        )
        copy.start()
        pending = [c for group in sent + halos for c in group]
        return jnp.concatenate(carry, axis=0), pending, copy

    def per_column(x):
        return jnp.sum(x, axis=0, keepdims=True)

    def folded(vector):
        width = cols
        return sum(vector[:, k * width : (k + 1) * width] for k in range(n_obs // width)) * 0.5

    def reduce_first(which, rows):
        red1[which, gx, 0:1, :] = rows[0]
        red1[which, gx, 1:2, :] = rows[1]
        copies = []
        for k in range(1, n_gx):
            copy = pltpu.make_async_remote_copy(
                src_ref=red1.at[which, gx],
                dst_ref=red1.at[which, gx],
                send_sem=red_send.at[which, 0, k],
                recv_sem=red_recv.at[which, 0, k],
                device_id=row_block(k),
                device_id_type=MESH,
            )
            copy.start()
            copies.append(copy)
        return copies

    def reduce_second(which, waits):
        for copy in waits:
            copy.wait_recv()
        red2[which, plane] = jnp.sum(red1[which], axis=0)
        copies = []
        for k in range(1, n_plane):
            copy = pltpu.make_async_remote_copy(
                src_ref=red2.at[which, plane],
                dst_ref=red2.at[which, plane],
                send_sem=red_send.at[which, 1, k],
                recv_sem=red_recv.at[which, 1, k],
                device_id=plane_device(k),
                device_id_type=MESH,
            )
            copy.start()
            copies.append(copy)
        return copies

    def reduce_last(which, waits):
        for copy in waits:
            copy.wait_recv()
        both = jnp.sum(jnp.sum(red2[which], axis=0), axis=1, keepdims=True)
        return both[0:1], both[1:2]

    grid_b, pending_b, p_copy_b = spread(0, scatter(innovation), lambda: None)
    gsum[ma] = gather(grid_b)
    g_copy = pltpu.make_async_remote_copy(
        src_ref=gsum.at[ma],
        dst_ref=gsum.at[ma],
        send_sem=g_sem.at[0],
        recv_sem=g_sem.at[1],
        device_id={"ma": other},
        device_id_type=MESH,
    )
    g_copy.start()
    first = reduce_first(
        0,
        (
            folded(innovation * innovation),
            per_column(
                sum(s_ref[0, x] * t_ref[0, x] for x in range(2))
            ) + folded(noise * innovation * innovation),
        ),
    )
    g_copy.wait()
    image = gsum[0] + gsum[1] + noise * innovation

    state = {}

    def meanwhile():
        state["second"] = reduce_second(0, first)

    grid_g, pending_g, p_copy_g = spread(1, scatter(image), meanwhile)
    norm_now, product = reduce_last(0, state["second"])
    alpha = norm_now / product
    residual = innovation - alpha * image
    along = per_column(
        sum(
            (s_ref[0, x] - alpha * s_ref[1, x]) * (t_ref[0, x] - alpha * t_ref[1, x])
            for x in range(2)
        )
    )
    last_first = reduce_first(
        1, (folded(residual * residual), along + folded(noise * residual * residual))
    )
    last_second = reduce_second(1, last_first)
    norm_next, product = reduce_last(1, last_second)
    ratio = norm_next / norm_now
    alpha_next = norm_next / (product - ratio * norm_next / alpha)
    weights = alpha * innovation + alpha_next * (residual + ratio * innovation)
    chosen = jnp.where(ma == 0, weights[:, : n_obs // 2], weights[:, n_obs // 2 :])
    w_ref[0:1, :] = chosen[:, :cols]
    w_ref[1:2, :] = chosen[:, cols:]

    p_copy_b.wait()
    p_copy_g.wait()
    first_weight = (alpha + alpha_next * (1.0 + ratio))[None]
    second_weight = (alpha * alpha_next)[None]
    inc_ref[...] = first_weight * (pmine[0, ma] + ptheirs[0]) - second_weight * (
        pmine[1, ma] + ptheirs[1]
    )

    for copy in pending_b + pending_g + first + state["second"] + last_first + last_second:
        copy.wait_send()


def shards(n_gx, n_gy, archive, obs_index, obs_value, obs_error):
    members, rows, levels, cols = archive.shape
    half = levels // 2
    n_own = obs_index.shape[0]
    piece = members // CHUNKS
    shape = (n_own // cols, cols)
    dma = pltpu.SemaphoreType.DMA
    vmem = pl.BlockSpec(memory_space=pltpu.VMEM)
    increment, weights = pl.pallas_call(
        functools.partial(kernel, n_gx, n_gy),
        out_shape=(
            jax.ShapeDtypeStruct((rows, half, cols), F32),
            jax.ShapeDtypeStruct(shape, F32),
        ),
        in_specs=[pl.BlockSpec(memory_space=pl.ANY), vmem, vmem, vmem],
        out_specs=(vmem, vmem),
        scratch_shapes=[
            pltpu.VMEM((members, rows, levels, cols), BF16),
            pltpu.VMEM((2, 8, cols), F32),
            pltpu.VMEM((2, rows * levels, cols), F32),
            pltpu.VMEM((rows, piece * 8, cols), F32),
            pltpu.VMEM((2, rows, members, cols), F32),
            pltpu.VMEM((2, rows, members, cols), F32),
            pltpu.VMEM((2, CHUNKS, rows, piece, cols), BF16),
            pltpu.VMEM((2, CHUNKS, len(NEAR), rows, piece, cols), BF16),
            pltpu.VMEM((2, CHUNKS, 2, piece, cols), BF16),
            pltpu.VMEM((2, CHUNKS, rows, piece, cols), F32),
            pltpu.VMEM((2, CHUNKS, rows, piece, cols), BF16),
            pltpu.VMEM((2, CHUNKS, 2, rows, piece, cols), BF16),
            pltpu.VMEM((6 * cols, cols), BF16),
            pltpu.VMEM((2, 2, rows, half, cols), F32),
            pltpu.VMEM((2, rows, half, cols), F32),
            pltpu.VMEM((2, 1, 2 * n_own), F32),
            pltpu.VMEM((2, n_gx, 2, cols), F32),
            pltpu.VMEM((2, 2 * n_gy, 2, cols), F32),
            dma((LOADS,)),
            dma((2,)),
            dma((2,)),
            dma((2, CHUNKS, len(NEAR))),
            dma((2, CHUNKS, len(NEAR))),
            dma((2, CHUNKS, 2)),
            dma((2, CHUNKS, 2)),
            dma((2, CHUNKS, 2)),
            dma((2, CHUNKS, 2)),
            dma((2, 2)),
            dma((2,)),
            dma((2, 2, max(n_gx, 2 * n_gy))),
            dma((2, 2, max(n_gx, 2 * n_gy))),
        ],
        compiler_params=pltpu.CompilerParams(
            collective_id=0, has_side_effects=True, vmem_limit_bytes=40 * 1024 * 1024
        ),
        name="analysis",
    )(archive, obs_index.reshape(shape), obs_value.reshape(shape), obs_error.reshape(shape))
    return increment, weights.reshape(n_own)


def solution(mesh):
    n_gx, n_gy = mesh.shape["gx"], mesh.shape["gy"]
    own = P(("gx", "gy", "ma"))
    return jax.shard_map(
        functools.partial(shards, n_gx, n_gy),
        mesh=mesh,
        in_specs=(P("ma", "gx", None, "gy"), own, own, own),
        out_specs=(P("gx", "ma", "gy"), own),
        check_vma=False,
    )
```

profile of v0, /device:TPU:1, one launch (start us, length us, event | category | flops | bytes accessed | tf_op | source)
XLA Modules:
  0.0 74.0 jit_solution(18396231161912661065)
XLA Ops:
  0.6 0.0 copy-start
  0.6 2.2 %copy-done = bf16[256,2,32,128]{3,2,1,0:T(8,128)(2,1)S(1)} copy-done((bf16[256,2,32,128]{3,2,1,0:T(8,128)(2,1)S(1)}, bf16[256,2,32,128]{3,2,1,0:T(8,128)(2,1)}, u32[]{:S(2)}) %copy-start) | copy-done | bytes 4194328
  2.8 0.0 copy-start.1
  2.8 0.7 copy-done.1
  3.5 0.0 copy-start.2
  3.5 0.7 copy-done.2
  4.2 0.0 copy-start.3
  4.2 0.7 copy-done.3
  4.9 68.0 %analysis.1 = (f32[2,16,128]{2,1,0:T(8,128)S(1)}, f32[2,128]{1,0:T(2,128)S(1)}) custom-call(bf16[256,2,32,128]{3,2,1,0:T(8,128)(2,1)S(1)} %copy-done, s32[2,128]{1,0:T(2,128)S(1)} %bitcast.4, f32[2,128]{1,0:T(2,128)S(1)} %bitcast.5, f32[2,128]{1,0:T(2,128)S(1)} %bitcast.6), custom_call_target="tpu_custom_call" | custom-call | tf_op jit(solution)/shard_map/analysis/pallas_call | solution.py:490
  72.9 0.6 copy.8
  73.5 0.6 copy.9
Async XLA Ops:
  0.6 2.2 %copy-start = (bf16[256,2,32,128]{3,2,1,0:T(8,128)(2,1)S(1)}, bf16[256,2,32,128]{3,2,1,0:T(8,128)(2,1)}, u32[]{:S(2)}) copy-start(bf16[256,2,32,128]{3,2,1,0:T(8,128)(2,1)} %archive_hbm.1) | copy-start | bytes 12582916
  2.8 0.7 copy-start.1
  3.5 0.7 copy-start.2
  4.2 0.7 copy-start.3
where the time goes:
time: 74.2 us; the launch traced here: 74 us
  Pallas kernels  68 us (92%)
  local copies, waits for them, and re-layouts  5.39 us (7%)
    pallas_call x1, Pallas kernels, shards(): pl.pallas_call(functools.partial(kernel, n_gx, n_gy), out_shape=(jax.Shap...  68 us
    unnamed x10, local copies, waits for them, and re-layouts  5.39 us

commit v1 on v0

v1 whole, which is shorter than its diff:
```python
import functools
import math

import jax
import jax.numpy as jnp
from jax import lax
from jax.experimental import pallas as pl
from jax.experimental.pallas import tpu as pltpu
from jax.sharding import PartitionSpec as P

M = 512
TAPER_X = 4
TAPER_Y = 8
F32 = jnp.float32
BF16 = jnp.bfloat16
MESH = pl.DeviceIdType.MESH

LOADS = 8
CHUNKS = 4
STRIP = 16
BOTH, BEFORE, AFTER, BESIDE, ONE = range(5)


def row_weight(distance):
    r = abs(distance) / TAPER_X
    if r <= 1.0:
        return (((-0.25 * r + 0.5) * r + 0.625) * r - 5.0 / 3.0) * r * r + 1.0
    if r < 2.0:
        return (
            ((((r / 12.0 - 0.5) * r + 0.625) * r + 5.0 / 3.0) * r - 5.0) * r
            + 4.0
            - 2.0 / (3.0 * r)
        )
    return 0.0


def taper_weight(distance, half_width):
    ratio = jnp.abs(distance) / half_width
    safe = jnp.maximum(ratio, 1.0)
    inner = (((-0.25 * ratio + 0.5) * ratio + 0.625) * ratio - 5.0 / 3.0) * ratio * ratio + 1.0
    outer = (
        ((((ratio / 12.0 - 0.5) * ratio + 0.625) * ratio + 5.0 / 3.0) * ratio - 5.0) * ratio
        + 4.0
        - 2.0 / (3.0 * safe)
    )
    return jnp.where(ratio <= 1.0, inner, jnp.where(ratio < 2.0, outer, 0.0))


def in_three(x):
    first = x.astype(BF16)
    rest = x - first.astype(F32)
    second = rest.astype(BF16)
    third = (rest - second.astype(F32)).astype(BF16)
    return jnp.concatenate([first, second, third], axis=0)


def sum_of_three(y, rows):
    return (y[2 * rows :] + y[rows : 2 * rows]) + y[:rows]


def kernel(
    n_gx,
    n_gy,
    archive_hbm,
    idx_hbm,
    val_hbm,
    err_hbm,
    inc_ref,
    w_ref,
    arch,
    idx_ref,
    val_ref,
    err_ref,
    meta,
    sums,
    part,
    s_ref,
    f_ref,
    h_ref,
    t_ref,
    out_ref,
    block_in,
    row_in,
    fwd_in,
    strip_out,
    strip_in,
    wcol,
    pmine,
    ptheirs,
    gsum,
    red1,
    red2,
    load_sem,
    meta_sem,
    sums_sem,
    block_send,
    block_recv,
    fwd_send,
    fwd_recv,
    strip_send,
    strip_recv,
    p_sem,
    g_sem,
    red_send,
    red_recv,
):
    members = arch.shape[0]
    levels = arch.shape[2]
    half = levels // 2
    cols = arch.shape[3]
    piece = members // CHUNKS
    gx = lax.axis_index("gx")
    gy = lax.axis_index("gy")
    ma = lax.axis_index("ma")
    core = lax.rem(gx, 2)
    other = 1 - ma
    plane = gy * 2 + ma
    n_plane = n_gy * 2

    def row_block(k):
        return {"gx": lax.rem(gx + (k + n_gx), n_gx)}

    def col_block(k):
        return {"gy": lax.rem(gy + (k + n_gy), n_gy)}

    def plane_device(k):
        at = lax.rem(plane + k, n_plane)
        return {"gy": at // 2, "ma": lax.rem(at, 2)}

    def remote(src, dst, send_sem, recv_sem, device):
        copy = pltpu.make_async_remote_copy(
            src_ref=src,
            dst_ref=dst,
            send_sem=send_sem,
            recv_sem=recv_sem,
            device_id=device,
            device_id_type=MESH,
        )
        copy.start()
        return copy

    barrier = pltpu.get_barrier_semaphore()
    for k in range(1, n_gx):
        pl.semaphore_signal(barrier, inc=1, device_id=row_block(k), device_id_type=MESH)
    for k in range(1, n_plane):
        pl.semaphore_signal(barrier, inc=1, device_id=plane_device(k), device_id_type=MESH)

    load = members // LOADS
    loads = []
    for k in range(LOADS):
        copy = pltpu.make_async_copy(
            archive_hbm.at[pl.ds(k * load, load)], arch.at[pl.ds(k * load, load)], load_sem.at[k]
        )
        copy.start()
        loads.append(copy)
    small = []
    for k, (src, dst) in enumerate(
        ((idx_hbm, idx_ref), (val_hbm, val_ref), (err_hbm, err_ref))
    ):
        copy = pltpu.make_async_copy(src, dst, load_sem.at[LOADS + k])
        copy.start()
        small.append(copy)

    source = lax.broadcasted_iota(jnp.int32, (cols, cols), 0)
    target = lax.broadcasted_iota(jnp.int32, (cols, cols), 1)

    def col_weight(shift):
        return taper_weight((source - target + shift).astype(F32), float(TAPER_Y))

    beside = jnp.where(gy > 0, col_weight(-cols), 0.0) + jnp.where(
        gy < n_gy - 1, col_weight(cols), 0.0
    )
    for k, weight in enumerate((col_weight(0), beside)):
        high = weight.astype(BF16)
        low = (weight - high.astype(F32)).astype(BF16)
        wcol[2 * k * cols : (2 * k + 1) * cols, :] = high
        wcol[(2 * k + 1) * cols : (2 * k + 2) * cols, :] = low
        if k == 0:
            wcol[4 * cols : 5 * cols, :] = high

    total = tuple(jnp.zeros((levels, cols), F32) for _ in range(2))
    for k in range(LOADS):
        loads[k].wait()

        def add(m, carry):
            return tuple(carry[x] + arch[m, x].astype(F32) for x in range(2))

        total = lax.fori_loop(k * load, (k + 1) * load, add, total, unroll=8)
    for x in range(2):
        sums[ma, x * levels : (x + 1) * levels, :] = total[x]
    for copy in small:
        copy.wait()
    meta[ma, 0:2, :] = idx_ref[...].astype(F32)
    meta[ma, 2:4, :] = val_ref[...]
    meta[ma, 4:6, :] = err_ref[...]
    meta[ma, 6:8, :] = jnp.zeros((2, cols), F32)

    pl.semaphore_wait(barrier, n_gx - 1 + n_plane - 1)

    partner = {"ma": other}
    meta_copy = remote(meta.at[ma], meta.at[ma], meta_sem.at[0], meta_sem.at[1], partner)
    sums_copy = remote(sums.at[ma], sums.at[ma], sums_sem.at[0], sums_sem.at[1], partner)

    meta_copy.wait()

    def in_a_row(first):
        rows = [meta[h, first + i : first + i + 1, :] for h in range(2) for i in range(2)]
        return jnp.concatenate(rows, axis=1)

    index = in_a_row(0).astype(jnp.int32)
    target_value = in_a_row(2)
    noise = in_a_row(4)
    n_obs = index.shape[1]
    owner = lax.broadcasted_iota(jnp.int32, (1, n_obs), 1) // (n_obs // 2)
    obs_line = (index >> 11) * levels + owner * half + ((index >> 7) & (half - 1))
    obs_col = index & (cols - 1)
    line_hot = (
        lax.broadcasted_iota(jnp.int32, (2 * levels, n_obs), 0) == obs_line
    ).astype(F32)
    col_hot = (
        (lax.broadcasted_iota(jnp.int32, (cols, n_obs), 0) == obs_col).astype(F32).astype(BF16)
    )

    def gather(grid):
        rows = 2 * levels
        spread = jnp.dot(in_three(grid), col_hot, preferred_element_type=F32)
        return jnp.sum(sum_of_three(spread, rows) * line_hot, axis=0, keepdims=True)

    def scatter(vector):
        rows = 2 * levels
        spread = lax.dot_general(
            in_three(line_hot * vector),
            col_hot,
            (((1,), (1,)), ((), ())),
            preferred_element_type=F32,
        )
        return sum_of_three(spread, rows)

    sums_copy.wait()
    average = (sums[0] + sums[1]) * (1.0 / M)
    innovation = target_value - gather(average)
    scale = 1.0 / math.sqrt(M - 1.0)

    def send_sources(phase, q):
        away = 8 * core - 4
        whole = out_ref.at[phase, q]

        def to(src, slot, dst, device):
            return remote(
                src, dst, block_send.at[phase, q, slot], block_recv.at[phase, q, slot], device
            )

        return {
            BOTH: to(whole, BOTH, block_in.at[phase, q, BOTH], row_block(away)),
            ONE: to(
                out_ref.at[phase, q, 1 - core], ONE, row_in.at[phase, q], row_block(-away)
            ),
            BEFORE: to(whole, BEFORE, block_in.at[phase, q, BEFORE], row_block(2)),
            AFTER: to(whole, AFTER, block_in.at[phase, q, AFTER], row_block(-2)),
            BESIDE: to(whole, BESIDE, block_in.at[phase, q, BESIDE], row_block(1 - 2 * core)),
        }

    def pass_on(phase, q, copies):
        passed = []
        for slot in (BEFORE, AFTER, BOTH):
            copies[slot].wait_recv()
            passed.append(
                remote(
                    block_in.at[phase, q, slot],
                    fwd_in.at[phase, q, slot],
                    fwd_send.at[phase, q, slot],
                    fwd_recv.at[phase, q, slot],
                    row_block(1 - 2 * core),
                )
            )
        return passed

    strip_rows = 2 * piece * STRIP // cols
    lane = lax.broadcasted_iota(jnp.int32, (strip_rows, cols), 1)

    def send_strips(phase, kind, q, field):
        last = first = jnp.zeros((strip_rows, cols), F32)
        for j in range(cols // STRIP):
            group = field[j * strip_rows : (j + 1) * strip_rows]
            mine = lane // STRIP == j
            last = jnp.where(mine, pltpu.roll(group, ((j + 1) * STRIP) % cols, 1), last)
            first = jnp.where(mine, pltpu.roll(group, j * STRIP, 1), first)
        copies = []
        for side, strip in enumerate((last, first)):
            strip_out[phase, kind, q, side] = strip.astype(BF16)
            copies.append(
                remote(
                    strip_out.at[phase, kind, q, side],
                    strip_in.at[phase, kind, q, side],
                    strip_send.at[phase, kind, q, side],
                    strip_recv.at[phase, kind, q, side],
                    col_block(1 - 2 * side),
                )
            )
        return copies

    def filter_cols(phase, kind, q, field, copies):
        for copy in copies:
            copy.wait_recv()
        left = strip_in[phase, kind, q, 0].astype(F32)
        right = strip_in[phase, kind, q, 1].astype(F32)
        strips = []
        for j in range(cols // STRIP):
            strips.append(
                jnp.where(
                    lane < cols // 2,
                    pltpu.roll(right, (cols - j * STRIP) % cols, 1),
                    pltpu.roll(left, cols - (j + 1) * STRIP, 1),
                )
            )
        strips = jnp.concatenate(strips, axis=0).astype(BF16)
        high = field.astype(BF16)
        low = (field - high.astype(F32)).astype(BF16)
        return jnp.dot(
            jnp.concatenate([high, high, strips, strips, low], axis=1),
            wcol[...],
            preferred_element_type=F32,
        )

    def form_sources(phase, q, grid):
        value = [grid[x * levels : (x + 1) * levels] for x in range(2)]
        mean = [average[x * levels : (x + 1) * levels] for x in range(2)]

        def one(i, carry):
            m = q * piece + i
            for x in range(2):
                if phase == 0:
                    anomaly = ((arch[m, x].astype(F32) - mean[x]) * scale).astype(BF16)
                    arch[m, x] = anomaly
                else:
                    anomaly = arch[m, x]
                product = anomaly.astype(F32) * value[x]
                part[x, pl.ds(pl.multiple_of(i * 8, 8), 8), :] = (
                    product[0:8] + product[8:16]
                ) + (product[16:24] + product[24:32])
            return carry

        lax.fori_loop(0, piece, one, 0, unroll=4)
        for x in range(2):
            for g in range(piece // 8):
                rows = [part[x, pl.ds(g * 64 + k, 8, stride=8), :] for k in range(8)]
                s_ref[phase, q, x * piece + g * 8 : x * piece + g * 8 + 8, :] = (
                    (rows[0] + rows[1]) + (rows[2] + rows[3])
                ) + ((rows[4] + rows[5]) + (rows[6] + rows[7]))
            out_ref[phase, q, x] = s_ref[phase, q, x * piece : (x + 1) * piece, :].astype(BF16)

    def filter_rows(phase, q, copies, passed):
        copies[BESIDE].wait_recv()
        copies[ONE].wait_recv()
        for copy in passed:
            copy.wait_recv()

        def weight(k, r, i):
            both = [row_weight(2 * at + r - i) for at in k]
            return both[0] if both[0] == both[1] else jnp.where(core == 0, both[0], both[1])

        blocks = [
            ((0, 0), lambda r: s_ref[phase, q, r * piece : (r + 1) * piece, :]),
            ((-2, -2), lambda r: block_in[phase, q, BEFORE, r].astype(F32)),
            ((2, 2), lambda r: block_in[phase, q, AFTER, r].astype(F32)),
            ((1, -1), lambda r: block_in[phase, q, BESIDE, r].astype(F32)),
            ((-1, -3), lambda r: fwd_in[phase, q, BEFORE, r].astype(F32)),
            ((3, 1), lambda r: fwd_in[phase, q, AFTER, r].astype(F32)),
            ((-3, 3), lambda r: fwd_in[phase, q, BOTH, r].astype(F32)),
        ]
        farthest = row_weight(7)
        far = [
            block_in[phase, q, BOTH, core].astype(F32) * farthest,
            row_in[phase, q].astype(F32) * farthest,
        ]
        outs = [jnp.where(core == 1, far[0], far[1]), jnp.where(core == 1, far[1], far[0])]
        for k, block in blocks:
            for r in range(2):
                row = block(r)
                for i in range(2):
                    outs[i] = outs[i] + row * weight(k, r, i)
        for i in range(2):
            f_ref[phase, q, i * piece : (i + 1) * piece, :] = outs[i]
        return send_strips(phase, 1, q, jnp.concatenate(outs, axis=0))

    def member_sum(phase, q, carry):
        def one(i, carry):
            m = q * piece + i
            return tuple(
                carry[x]
                + arch[m, x].astype(F32) * t_ref[q, pl.ds(x * piece + i, 1), :]
                for x in range(2)
            )

        return lax.fori_loop(0, piece, one, carry, unroll=4)

    def spread(phase, grid, meanwhile, rows_done):
        pending = []
        sent, own_strips, passed, strips = [], [], [], []
        for q in range(CHUNKS):
            form_sources(phase, q, grid)
            sent.append(send_sources(phase, q))
            own_strips.append(send_strips(phase, 0, q, s_ref[phase, q]))
        meanwhile()
        carry = tuple(jnp.zeros((levels, cols), F32) for _ in range(2))

        def finish(q, carry):
            t_ref[q] = filter_cols(phase, 1, q, f_ref[phase, q], strips[q])
            return member_sum(phase, q, carry)

        for q in range(CHUNKS + 1):
            if q < CHUNKS:
                h_ref[phase, q] = filter_cols(phase, 0, q, s_ref[phase, q], own_strips[q])
                passed.append(pass_on(phase, q, sent[q]))
            if q >= 1:
                strips.append(filter_rows(phase, q - 1, sent[q - 1], passed[q - 1]))
            if q >= 3 and q < CHUNKS:
                carry = finish(q - 3, carry)
        rows_done()
        for q in range(max(CHUNKS - 3, 0), CHUNKS):
            carry = finish(q, carry)
        for x in range(2):
            for h in range(2):
                pmine[phase, h, x] = carry[x][h * half : (h + 1) * half]
        pending = [c for group in sent for c in group.values()]
        pending += [c for group in own_strips + passed + strips for c in group]
        return jnp.concatenate(carry, axis=0), pending

    def send_increment(phase):
        return remote(
            pmine.at[phase, other], ptheirs.at[phase], p_sem.at[phase, 0], p_sem.at[phase, 1], partner
        )

    def per_column(x):
        return jnp.sum(x, axis=0, keepdims=True)

    def folded(vector):
        return (
            sum(vector[:, k * cols : (k + 1) * cols] for k in range(n_obs // cols)) * 0.5
        )

    def reduce_first(which, rows):
        red1[which, gx, 0:1, :] = rows[0]
        red1[which, gx, 1:2, :] = rows[1]
        mine = red1.at[which, gx]
        return [
            remote(mine, mine, red_send.at[which, 0, k], red_recv.at[which, 0, k], row_block(k))
            for k in range(1, n_gx)
        ]

    def reduce_second(which, waits):
        for copy in waits:
            copy.wait_recv()
        red2[which, plane] = jnp.sum(red1[which], axis=0)
        mine = red2.at[which, plane]
        return [
            remote(mine, mine, red_send.at[which, 1, k], red_recv.at[which, 1, k], plane_device(k))
            for k in range(1, n_plane)
        ]

    def reduce_last(which, waits):
        for copy in waits:
            copy.wait_recv()
        both = jnp.sum(jnp.sum(red2[which], axis=0), axis=1, keepdims=True)
        return both[0:1], both[1:2]

    state = {}

    def nothing():
        pass

    grid_b, pending_b = spread(0, scatter(innovation), nothing, nothing)
    gsum[ma] = gather(grid_b)
    g_copy = remote(gsum.at[ma], gsum.at[ma], g_sem.at[0], g_sem.at[1], partner)
    p_copy_b = send_increment(0)
    along = per_column(sum(f_ref[0, q] * h_ref[0, q] for q in range(CHUNKS)))
    first = reduce_first(
        0,
        (
            folded(innovation * innovation),
            along + folded(noise * innovation * innovation),
        ),
    )
    g_copy.wait()
    image = gsum[0] + gsum[1] + noise * innovation

    def meanwhile():
        state["second"] = reduce_second(0, first)

    def rows_done():
        norm_now, product = reduce_last(0, state["second"])
        alpha = norm_now / product
        residual = innovation - alpha * image
        along = per_column(
            sum(
                (f_ref[0, q] - alpha * f_ref[1, q]) * (h_ref[0, q] - alpha * h_ref[1, q])
                for q in range(CHUNKS)
            )
        )
        state["last_first"] = reduce_first(
            1, (folded(residual * residual), along + folded(noise * residual * residual))
        )
        state["step"] = norm_now, alpha, residual

    grid_g, pending_g = spread(1, scatter(image), meanwhile, rows_done)
    p_copy_g = send_increment(1)
    norm_now, alpha, residual = state["step"]
    last_second = reduce_second(1, state["last_first"])
    norm_next, product = reduce_last(1, last_second)
    ratio = norm_next / norm_now
    alpha_next = norm_next / (product - ratio * norm_next / alpha)
    weights = alpha * innovation + alpha_next * (residual + ratio * innovation)
    chosen = jnp.where(ma == 0, weights[:, : n_obs // 2], weights[:, n_obs // 2 :])
    w_ref[0:1, :] = chosen[:, :cols]
    w_ref[1:2, :] = chosen[:, cols:]

    p_copy_b.wait()
    p_copy_g.wait()
    first_weight = (alpha + alpha_next * (1.0 + ratio))[None]
    second_weight = (alpha * alpha_next)[None]
    inc_ref[...] = first_weight * (pmine[0, ma] + ptheirs[0]) - second_weight * (
        pmine[1, ma] + ptheirs[1]
    )

    for copy in (
        pending_b
        + pending_g
        + first
        + state["second"]
        + state["last_first"]
        + last_second
    ):
        copy.wait_send()


def shards(n_gx, n_gy, archive, obs_index, obs_value, obs_error):
    members, rows, levels, cols = archive.shape
    half = levels // 2
    n_own = obs_index.shape[0]
    piece = members // CHUNKS
    strip_rows = rows * piece * STRIP // cols
    shape = (n_own // cols, cols)
    dma = pltpu.SemaphoreType.DMA
    vmem = pl.BlockSpec(memory_space=pltpu.VMEM)
    hbm = pl.BlockSpec(memory_space=pl.ANY)
    increment, weights = pl.pallas_call(
        functools.partial(kernel, n_gx, n_gy),
        out_shape=(
            jax.ShapeDtypeStruct((rows, half, cols), F32),
            jax.ShapeDtypeStruct(shape, F32),
        ),
        in_specs=[hbm, hbm, hbm, hbm],
        out_specs=(vmem, vmem),
        scratch_shapes=[
            pltpu.VMEM((members, rows, levels, cols), BF16),
            pltpu.VMEM(shape, jnp.int32),
            pltpu.VMEM(shape, F32),
            pltpu.VMEM(shape, F32),
            pltpu.VMEM((2, 8, cols), F32),
            pltpu.VMEM((2, rows * levels, cols), F32),
            pltpu.VMEM((rows, piece * 8, cols), F32),
            pltpu.VMEM((2, CHUNKS, rows * piece, cols), F32),
            pltpu.VMEM((2, CHUNKS, rows * piece, cols), F32),
            pltpu.VMEM((2, CHUNKS, rows * piece, cols), F32),
            pltpu.VMEM((CHUNKS, rows * piece, cols), F32),
            pltpu.VMEM((2, CHUNKS, rows, piece, cols), BF16),
            pltpu.VMEM((2, CHUNKS, 4, rows, piece, cols), BF16),
            pltpu.VMEM((2, CHUNKS, piece, cols), BF16),
            pltpu.VMEM((2, CHUNKS, 3, rows, piece, cols), BF16),
            pltpu.VMEM((2, 2, CHUNKS, 2, strip_rows, cols), BF16),
            pltpu.VMEM((2, 2, CHUNKS, 2, strip_rows, cols), BF16),
            pltpu.VMEM((5 * cols, cols), BF16),
            pltpu.VMEM((2, 2, rows, half, cols), F32),
            pltpu.VMEM((2, rows, half, cols), F32),
            pltpu.VMEM((2, 1, 2 * n_own), F32),
            pltpu.VMEM((2, n_gx, 2, cols), F32),
            pltpu.VMEM((2, 2 * n_gy, 2, cols), F32),
            dma((LOADS + 3,)),
            dma((2,)),
            dma((2,)),
            dma((2, CHUNKS, 5)),
            dma((2, CHUNKS, 5)),
            dma((2, CHUNKS, 3)),
            dma((2, CHUNKS, 3)),
            dma((2, 2, CHUNKS, 2)),
            dma((2, 2, CHUNKS, 2)),
            dma((2, 2)),
            dma((2,)),
            dma((2, 2, max(n_gx, 2 * n_gy))),
            dma((2, 2, max(n_gx, 2 * n_gy))),
        ],
        compiler_params=pltpu.CompilerParams(
            collective_id=0, has_side_effects=True, vmem_limit_bytes=60 * 1024 * 1024
        ),
        name="analysis",
    )(archive, obs_index.reshape(shape), obs_value.reshape(shape), obs_error.reshape(shape))
    return increment, weights.reshape(n_own)


def solution(mesh):
    n_gx, n_gy = mesh.shape["gx"], mesh.shape["gy"]
    own = P(("gx", "gy", "ma"))
    return jax.shard_map(
        functools.partial(shards, n_gx, n_gy),
        mesh=mesh,
        in_specs=(P("ma", "gx", None, "gy"), own, own, own),
        out_specs=(P("gx", "ma", "gy"), own),
        check_vma=False,
    )
```

time: 74.2 us -> 61 us (0.82)
  Pallas kernels: 68 us -> 57.7 us
  local copies, waits for them, and re-layouts: 5.39 us -> 2.54 us
    pallas_call x1, Pallas kernels: 68 us -> 57.7 us  [shards(): pl.pallas_call(functools.partial(kernel, n_gx, n_gy), out_shape=(jax.Shap...]
    unnamed x10 -> x2, local copies, waits for them, and re-layouts: 5.39 us -> 2.54 us
where the time goes in v1:
time: 61 us; the launch traced here: 60.8 us
  Pallas kernels  57.7 us (95%)
  local copies, waits for them, and re-layouts  2.54 us (4%)
  between operations  0.64 us (1%)
    pallas_call x1, Pallas kernels, shards(): pl.pallas_call(functools.partial(kernel, n_gx, n_gy), out_shape=(jax.Shap...  57.7 us
    unnamed x2, local copies, waits for them, and re-layouts  2.54 us

profile of v1, /device:TPU:1, one launch (start us, length us, event | category | flops | bytes accessed | tf_op | source)
XLA Modules:
  0.0 60.8 jit_solution(11069848080824713665)
XLA Ops:
  0.6 57.7 %analysis.1 = (f32[2,16,128]{2,1,0:T(8,128)}, f32[2,128]{1,0:T(2,128)}) custom-call(bf16[256,2,32,128]{3,2,1,0:T(8,128)(2,1)} %archive_hbm.1, s32[2,128]{1,0:T(2,128)} %bitcast.4, f32[2,128]{1,0:T(2,128)} %bitcast.5, f32[2,128]{1,0:T(2,128)} %bitcast.6), custom_call_target="tpu_custom_call" | custom-call | tf_op jit(solution)/shard_map/analysis/pallas_call | solution.py:546
  58.3 1.3 %copy.8 = f32[2,16,128]{2,1,0:T(8,128)} copy(f32[2,16,128]{2,1,0:T(8,128)} %get-tuple-element.8) | data formatting | bytes 32768
  59.6 1.2 %copy.9 = f32[256]{0:T(256)} copy(f32[256]{0:T(256)} %bitcast.7) | data formatting | bytes 2048

commit v2 on v1

--- a/solution.py
+++ b/solution.py
@@ -16,6 +16,8 @@
 MESH = pl.DeviceIdType.MESH
 
 LOADS = 8
+ROWS_FIRST = (0, 1)
+COLS_FIRST = (2, 3)
 CHUNKS = 4
 STRIP = 16
 BOTH, BEFORE, AFTER, BESIDE, ONE = range(5)
@@ -241,7 +243,9 @@
     innovation = target_value - gather(average)
     scale = 1.0 / math.sqrt(M - 1.0)
 
-    def send_sources(phase, q):
+    def send_sources(phase, q, field):
+        for x in range(2):
+            out_ref[phase, q, x] = field[x * piece : (x + 1) * piece].astype(BF16)
         away = 8 * core - 4
         whole = out_ref.at[phase, q]
 
@@ -347,9 +351,8 @@
                 s_ref[phase, q, x * piece + g * 8 : x * piece + g * 8 + 8, :] = (
                     (rows[0] + rows[1]) + (rows[2] + rows[3])
                 ) + ((rows[4] + rows[5]) + (rows[6] + rows[7]))
-            out_ref[phase, q, x] = s_ref[phase, q, x * piece : (x + 1) * piece, :].astype(BF16)
-
-    def filter_rows(phase, q, copies, passed):
+
+    def filter_rows(phase, q, own, copies, passed):
         copies[BESIDE].wait_recv()
         copies[ONE].wait_recv()
         for copy in passed:
@@ -360,7 +363,7 @@
             return both[0] if both[0] == both[1] else jnp.where(core == 0, both[0], both[1])
 
         blocks = [
-            ((0, 0), lambda r: s_ref[phase, q, r * piece : (r + 1) * piece, :]),
+            ((0, 0), lambda r: own[phase, q, r * piece : (r + 1) * piece, :]),
             ((-2, -2), lambda r: block_in[phase, q, BEFORE, r].astype(F32)),
             ((2, 2), lambda r: block_in[phase, q, AFTER, r].astype(F32)),
             ((1, -1), lambda r: block_in[phase, q, BESIDE, r].astype(F32)),
@@ -379,60 +382,74 @@
                 row = block(r)
                 for i in range(2):
                     outs[i] = outs[i] + row * weight(k, r, i)
-        for i in range(2):
-            f_ref[phase, q, i * piece : (i + 1) * piece, :] = outs[i]
-        return send_strips(phase, 1, q, jnp.concatenate(outs, axis=0))
+        return jnp.concatenate(outs, axis=0)
 
     def member_sum(phase, q, carry):
         def one(i, carry):
             m = q * piece + i
             return tuple(
                 carry[x]
-                + arch[m, x].astype(F32) * t_ref[q, pl.ds(x * piece + i, 1), :]
+                + arch[m, x].astype(F32) * t_ref[phase, q, pl.ds(x * piece + i, 1), :]
                 for x in range(2)
             )
 
         return lax.fori_loop(0, piece, one, carry, unroll=4)
 
     def spread(phase, grid, meanwhile, rows_done):
-        pending = []
-        sent, own_strips, passed, strips = [], [], [], []
+        sent, own_strips, passed, strips = {}, {}, {}, {}
+        for pair in zip(ROWS_FIRST, COLS_FIRST):
+            for q in pair:
+                form_sources(phase, q, grid)
+                if q in ROWS_FIRST:
+                    sent[q] = send_sources(phase, q, s_ref[phase, q])
+                own_strips[q] = send_strips(phase, 0, q, s_ref[phase, q])
+        meanwhile()
+        for q in COLS_FIRST:
+            h_ref[phase, q] = filter_cols(phase, 0, q, s_ref[phase, q], own_strips[q])
+            sent[q] = send_sources(phase, q, h_ref[phase, q])
+        for q in ROWS_FIRST:
+            h_ref[phase, q] = filter_cols(phase, 0, q, s_ref[phase, q], own_strips[q])
+
+        def rows_of(q):
+            if q in ROWS_FIRST:
+                f_ref[phase, q] = filter_rows(phase, q, s_ref, sent[q], passed[q])
+                strips[q] = send_strips(phase, 1, q, f_ref[phase, q])
+            else:
+                t_ref[phase, q] = filter_rows(phase, q, h_ref, sent[q], passed[q])
+
+        def finish(q, carry):
+            if q in ROWS_FIRST:
+                t_ref[phase, q] = filter_cols(phase, 1, q, f_ref[phase, q], strips[q])
+            return member_sum(phase, q, carry)
+
+        carry = tuple(jnp.zeros((levels, cols), F32) for _ in range(2))
         for q in range(CHUNKS):
-            form_sources(phase, q, grid)
-            sent.append(send_sources(phase, q))
-            own_strips.append(send_strips(phase, 0, q, s_ref[phase, q]))
-        meanwhile()
-        carry = tuple(jnp.zeros((levels, cols), F32) for _ in range(2))
-
-        def finish(q, carry):
-            t_ref[q] = filter_cols(phase, 1, q, f_ref[phase, q], strips[q])
-            return member_sum(phase, q, carry)
-
-        for q in range(CHUNKS + 1):
-            if q < CHUNKS:
-                h_ref[phase, q] = filter_cols(phase, 0, q, s_ref[phase, q], own_strips[q])
-                passed.append(pass_on(phase, q, sent[q]))
+            passed[q] = pass_on(phase, q, sent[q])
             if q >= 1:
-                strips.append(filter_rows(phase, q - 1, sent[q - 1], passed[q - 1]))
-            if q >= 3 and q < CHUNKS:
-                carry = finish(q - 3, carry)
+                rows_of(q - 1)
+        carry = finish(0, carry)
+        carry = finish(2, carry)
+        rows_of(CHUNKS - 1)
         rows_done()
-        for q in range(max(CHUNKS - 3, 0), CHUNKS):
-            carry = finish(q, carry)
+        carry = finish(1, carry)
+        carry = finish(3, carry)
         for x in range(2):
             for h in range(2):
                 pmine[phase, h, x] = carry[x][h * half : (h + 1) * half]
-        pending = [c for group in sent for c in group.values()]
-        pending += [c for group in own_strips + passed + strips for c in group]
+        pending = [c for group in sent.values() for c in group.values()]
+        for groups in (own_strips, passed, strips):
+            pending += [c for group in groups.values() for c in group]
         return jnp.concatenate(carry, axis=0), pending
+
+    def dotted(left, right):
+        terms = [left(f_ref, q) * right(h_ref, q) for q in ROWS_FIRST]
+        terms += [left(s_ref, q) * right(t_ref, q) for q in COLS_FIRST]
+        return jnp.sum(sum(terms), axis=0, keepdims=True)
 
     def send_increment(phase):
         return remote(
             pmine.at[phase, other], ptheirs.at[phase], p_sem.at[phase, 0], p_sem.at[phase, 1], partner
         )
-
-    def per_column(x):
-        return jnp.sum(x, axis=0, keepdims=True)
 
     def folded(vector):
         return (
@@ -473,7 +490,7 @@
     gsum[ma] = gather(grid_b)
     g_copy = remote(gsum.at[ma], gsum.at[ma], g_sem.at[0], g_sem.at[1], partner)
     p_copy_b = send_increment(0)
-    along = per_column(sum(f_ref[0, q] * h_ref[0, q] for q in range(CHUNKS)))
+    along = dotted(lambda ref, q: ref[0, q], lambda ref, q: ref[0, q])
     first = reduce_first(
         0,
         (
@@ -491,12 +508,11 @@
         norm_now, product = reduce_last(0, state["second"])
         alpha = norm_now / product
         residual = innovation - alpha * image
-        along = per_column(
-            sum(
-                (f_ref[0, q] - alpha * f_ref[1, q]) * (h_ref[0, q] - alpha * h_ref[1, q])
-                for q in range(CHUNKS)
-            )
-        )
+
+        def of_residual(ref, q):
+            return ref[0, q] - alpha * ref[1, q]
+
+        along = dotted(of_residual, of_residual)
         state["last_first"] = reduce_first(
             1, (folded(residual * residual), along + folded(noise * residual * residual))
         )
@@ -506,6 +522,9 @@
     p_copy_g = send_increment(1)
     norm_now, alpha, residual = state["step"]
     last_second = reduce_second(1, state["last_first"])
+    for copy in pending_b + pending_g + first + state["second"] + state["last_first"]:
+        copy.wait_send()
+    p_copy_b.wait()
     norm_next, product = reduce_last(1, last_second)
     ratio = norm_next / norm_now
     alpha_next = norm_next / (product - ratio * norm_next / alpha)
@@ -514,7 +533,6 @@
     w_ref[0:1, :] = chosen[:, :cols]
     w_ref[1:2, :] = chosen[:, cols:]
 
-    p_copy_b.wait()
     p_copy_g.wait()
     first_weight = (alpha + alpha_next * (1.0 + ratio))[None]
     second_weight = (alpha * alpha_next)[None]
@@ -522,14 +540,7 @@
         pmine[1, ma] + ptheirs[1]
     )
 
-    for copy in (
-        pending_b
-        + pending_g
-        + first
-        + state["second"]
-        + state["last_first"]
-        + last_second
-    ):
+    for copy in last_second:
         copy.wait_send()
 
 
@@ -542,12 +553,12 @@
     shape = (n_own // cols, cols)
     dma = pltpu.SemaphoreType.DMA
     vmem = pl.BlockSpec(memory_space=pltpu.VMEM)
-    hbm = pl.BlockSpec(memory_space=pl.ANY)
+    hbm = pl.BlockSpec(memory_space=pltpu.HBM)
     increment, weights = pl.pallas_call(
         functools.partial(kernel, n_gx, n_gy),
         out_shape=(
-            jax.ShapeDtypeStruct((rows, half, cols), F32),
-            jax.ShapeDtypeStruct(shape, F32),
+            pltpu.VMEM((rows, half, cols), F32),
+            pltpu.VMEM(shape, F32),
         ),
         in_specs=[hbm, hbm, hbm, hbm],
         out_specs=(vmem, vmem),
@@ -562,7 +573,7 @@
             pltpu.VMEM((2, CHUNKS, rows * piece, cols), F32),
             pltpu.VMEM((2, CHUNKS, rows * piece, cols), F32),
             pltpu.VMEM((2, CHUNKS, rows * piece, cols), F32),
-            pltpu.VMEM((CHUNKS, rows * piece, cols), F32),
+            pltpu.VMEM((2, CHUNKS, rows * piece, cols), F32),
             pltpu.VMEM((2, CHUNKS, rows, piece, cols), BF16),
             pltpu.VMEM((2, CHUNKS, 4, rows, piece, cols), BF16),
             pltpu.VMEM((2, CHUNKS, piece, cols), BF16),
@@ -590,7 +601,7 @@
             dma((2, 2, max(n_gx, 2 * n_gy))),
         ],
         compiler_params=pltpu.CompilerParams(
-            collective_id=0, has_side_effects=True, vmem_limit_bytes=60 * 1024 * 1024
+            collective_id=0, has_side_effects=True, vmem_limit_bytes=56 * 1024 * 1024
         ),
         name="analysis",
     )(archive, obs_index.reshape(shape), obs_value.reshape(shape), obs_error.reshape(shape))

time: 61 us -> 57.7 us (0.946)
  Pallas kernels: 57.7 us -> 55.8 us
  local copies, waits for them, and re-layouts: 2.54 us -> 1.17 us
    pallas_call x1, Pallas kernels: 57.7 us -> 55.8 us  [shards(): pl.pallas_call(functools.partial(kernel, n_gx, n_gy), out_shape=(pltpu.VM...]
    unnamed x2, local copies, waits for them, and re-layouts: 2.54 us -> 1.17 us
where the time goes in v2:
time: 57.7 us
  Pallas kernels  55.8 us (97%)
  local copies, waits for them, and re-layouts  1.17 us (2%)
  between operations  0.64 us (1%)
    pallas_call x1, Pallas kernels, shards(): pl.pallas_call(functools.partial(kernel, n_gx, n_gy), out_shape=(pltpu.VM...  55.8 us
    unnamed x2, local copies, waits for them, and re-layouts  1.17 us

profile of v2, /device:TPU:1, one launch (start us, length us, event | category | flops | bytes accessed | tf_op | source)
XLA Modules:
  0.0 57.7 jit_solution(4613022293117732106)
XLA Ops:
  0.6 55.8 %analysis.1 = (f32[2,16,128]{2,1,0:T(8,128)S(1)}, f32[2,128]{1,0:T(2,128)S(1)}) custom-call(bf16[256,2,32,128]{3,2,1,0:T(8,128)(2,1)} %archive_hbm.1, s32[2,128]{1,0:T(2,128)} %bitcast.5, f32[2,128]{1,0:T(2,128)} %bitcast.6, f32[2,128]{1,0:T(2,128)} %bitcast.7), custom_call_target="tpu_custom_call" | custom-call | tf_op jit(solution)/shard_map/analysis/pallas_call | solution.py:557
  56.5 0.6 %copy.8 = f32[2,16,128]{2,1,0:T(8,128)} copy(f32[2,16,128]{2,1,0:T(8,128)S(1)} %get-tuple-element.6) | data formatting | bytes 32768
  57.1 0.6 copy.9

commit v3 on v1

v3 whole, which is shorter than its diff:
```python
import functools
import math

import jax
import jax.numpy as jnp
from jax import lax
from jax.experimental import pallas as pl
from jax.experimental.pallas import tpu as pltpu
from jax.sharding import PartitionSpec as P

M = 512
TAPER_X = 4
TAPER_Y = 8
F32 = jnp.float32
BF16 = jnp.bfloat16
MESH = pl.DeviceIdType.MESH

LOADS = 8
CHUNKS = 4
ORDER = (0, 2, 1, 3)
STRIP = 16
SOURCE, FILTERED = 0, 1


def course(kind, q):
    return (1 if q < CHUNKS // 2 else -1) * (1 if kind == SOURCE else -1)


def row_weight(distance):
    r = abs(distance) / TAPER_X
    if r <= 1.0:
        return (((-0.25 * r + 0.5) * r + 0.625) * r - 5.0 / 3.0) * r * r + 1.0
    if r < 2.0:
        return (
            ((((r / 12.0 - 0.5) * r + 0.625) * r + 5.0 / 3.0) * r - 5.0) * r
            + 4.0
            - 2.0 / (3.0 * r)
        )
    return 0.0


def taper_weight(distance, half_width):
    ratio = jnp.abs(distance) / half_width
    safe = jnp.maximum(ratio, 1.0)
    inner = (((-0.25 * ratio + 0.5) * ratio + 0.625) * ratio - 5.0 / 3.0) * ratio * ratio + 1.0
    outer = (
        ((((ratio / 12.0 - 0.5) * ratio + 0.625) * ratio + 5.0 / 3.0) * ratio - 5.0) * ratio
        + 4.0
        - 2.0 / (3.0 * safe)
    )
    return jnp.where(ratio <= 1.0, inner, jnp.where(ratio < 2.0, outer, 0.0))


def in_three(x):
    first = x.astype(BF16)
    rest = x - first.astype(F32)
    second = rest.astype(BF16)
    third = (rest - second.astype(F32)).astype(BF16)
    return jnp.concatenate([first, second, third], axis=0)


def sum_of_three(y, rows):
    return (y[2 * rows :] + y[rows : 2 * rows]) + y[:rows]


def kernel(
    n_gx,
    n_gy,
    archive_hbm,
    idx_hbm,
    val_hbm,
    err_hbm,
    inc_ref,
    w_ref,
    arch,
    idx_ref,
    pair_ref,
    meta,
    sums,
    part,
    s_ref,
    f_ref,
    h_ref,
    t_ref,
    out_ref,
    side_in,
    beside_in,
    sent_ref,
    strip_out,
    strip_in,
    wcol,
    pmine,
    ptheirs,
    gsum,
    red1,
    red2,
    load_sem,
    meta_sem,
    sums_sem,
    block_send,
    block_recv,
    fwd_recv,
    beside_recv,
    strip_send,
    strip_recv,
    p_sem,
    g_sem,
    red_send,
    red_recv,
):
    members = arch.shape[0]
    levels = arch.shape[2]
    half = levels // 2
    cols = arch.shape[3]
    piece = members // CHUNKS
    gx = lax.axis_index("gx")
    gy = lax.axis_index("gy")
    ma = lax.axis_index("ma")
    core = lax.rem(gx, 2)
    other = 1 - ma
    sent_rows = sent_ref.at[0 : 15 * CHUNKS]
    plane = gy * 2 + ma
    n_plane = n_gy * 2

    def row_block(k):
        return {"gx": lax.rem(gx + (k + n_gx), n_gx)}

    def col_block(k):
        return {"gy": lax.rem(gy + (k + n_gy), n_gy)}

    def plane_device(k):
        at = lax.rem(plane + k, n_plane)
        return {"gy": at // 2, "ma": lax.rem(at, 2)}

    def remote(src, dst, send_sem, recv_sem, device):
        copy = pltpu.make_async_remote_copy(
            src_ref=src,
            dst_ref=dst,
            send_sem=send_sem,
            recv_sem=recv_sem,
            device_id=device,
            device_id_type=MESH,
        )
        copy.start()
        return copy

    def wait_for(ref, sem):
        pltpu.make_async_copy(ref, ref, sem).wait()

    load = members // LOADS
    loads = []
    for k in range(LOADS):
        copy = pltpu.make_async_copy(
            archive_hbm.at[pl.ds(k * load, load)], arch.at[pl.ds(k * load, load)], load_sem.at[k]
        )
        copy.start()
        loads.append(copy)
    pltpu.make_async_copy(idx_hbm, idx_ref, load_sem.at[LOADS]).start()
    pltpu.make_async_copy(val_hbm, pair_ref.at[0], load_sem.at[LOADS + 1]).start()
    pltpu.make_async_copy(err_hbm, pair_ref.at[1], load_sem.at[LOADS + 1]).start()

    barrier = pltpu.get_barrier_semaphore()
    for k in range(1, n_gx):
        pl.semaphore_signal(barrier, inc=1, device_id=row_block(k), device_id_type=MESH)
    for k in range(1, n_plane):
        pl.semaphore_signal(barrier, inc=1, device_id=plane_device(k), device_id_type=MESH)

    source = lax.broadcasted_iota(jnp.int32, (cols, cols), 0)
    target = lax.broadcasted_iota(jnp.int32, (cols, cols), 1)

    def col_weight(shift):
        return taper_weight((source - target + shift).astype(F32), float(TAPER_Y))

    beside = jnp.where(gy > 0, col_weight(-cols), 0.0) + jnp.where(
        gy < n_gy - 1, col_weight(cols), 0.0
    )
    for k, weight in enumerate((col_weight(0), beside)):
        high = weight.astype(BF16)
        low = (weight - high.astype(F32)).astype(BF16)
        wcol[2 * k * cols : (2 * k + 1) * cols, :] = high
        wcol[(2 * k + 1) * cols : (2 * k + 2) * cols, :] = low
        if k == 0:
            wcol[4 * cols : 5 * cols, :] = high

    total = tuple(jnp.zeros((levels, cols), F32) for _ in range(2))
    for k in range(LOADS):
        loads[k].wait()

        def add(m, carry):
            return tuple(carry[x] + arch[m, x].astype(F32) for x in range(2))

        total = lax.fori_loop(k * load, (k + 1) * load, add, total, unroll=8)
    for x in range(2):
        sums[ma, x * levels : (x + 1) * levels, :] = total[x]
    wait_for(idx_ref, load_sem.at[LOADS])
    wait_for(pair_ref, load_sem.at[LOADS + 1])
    meta[ma, 0:2, :] = idx_ref[...].astype(F32)
    meta[ma, 2:4, :] = pair_ref[0]
    meta[ma, 4:6, :] = pair_ref[1]
    meta[ma, 6:8, :] = jnp.zeros((2, cols), F32)

    pl.semaphore_wait(barrier, n_gx - 1 + n_plane - 1)

    partner = {"ma": other}
    meta_copy = remote(meta.at[ma], meta.at[ma], meta_sem.at[0], meta_sem.at[1], partner)
    sums_copy = remote(sums.at[ma], sums.at[ma], sums_sem.at[0], sums_sem.at[1], partner)

    meta_copy.wait()

    def in_a_row(first):
        rows = [meta[h, first + i : first + i + 1, :] for h in range(2) for i in range(2)]
        return jnp.concatenate(rows, axis=1)

    index = in_a_row(0).astype(jnp.int32)
    target_value = in_a_row(2)
    noise = in_a_row(4)
    n_obs = index.shape[1]
    owner = lax.broadcasted_iota(jnp.int32, (1, n_obs), 1) // (n_obs // 2)
    obs_line = (index >> 11) * levels + owner * half + ((index >> 7) & (half - 1))
    obs_col = index & (cols - 1)
    line_hot = (
        lax.broadcasted_iota(jnp.int32, (2 * levels, n_obs), 0) == obs_line
    ).astype(F32)
    col_hot = (
        (lax.broadcasted_iota(jnp.int32, (cols, n_obs), 0) == obs_col).astype(F32).astype(BF16)
    )

    def gather(grid):
        rows = 2 * levels
        spread = jnp.dot(in_three(grid), col_hot, preferred_element_type=F32)
        return jnp.sum(sum_of_three(spread, rows) * line_hot, axis=0, keepdims=True)

    def scatter(vector):
        rows = 2 * levels
        spread = lax.dot_general(
            in_three(line_hot * vector),
            col_hot,
            (((1,), (1,)), ((), ())),
            preferred_element_type=F32,
        )
        return sum_of_three(spread, rows)

    sums_copy.wait()
    average = (sums[0] + sums[1]) * (1.0 / M)
    innovation = target_value - gather(average)
    scale = 1.0 / math.sqrt(M - 1.0)

    beside_me = row_block(1 - 2 * core)

    def big(way):
        return core == (1 if way > 0 else 0)

    def send_block(phase, kind, q, field):
        way = course(kind, q)
        row = 1 if way > 0 else 0
        for x in range(2):
            out_ref[phase, kind, q, x] = field[x * piece : (x + 1) * piece].astype(BF16)
        block = out_ref.at[phase, kind, q]
        here = side_in.at[phase, kind, q]
        sems = block_send.at[phase], block_recv.at[phase, kind, q]

        @pl.when(big(way))
        def _():
            remote(block, here.at[2:4], *sems, row_block(4 * way))

        @pl.when(jnp.logical_not(big(way)))
        def _():
            remote(block.at[row], here.at[2], *sems, row_block(4 * way))

        remote(block, here.at[0:2], *sems, row_block(2 * way))

    def either(way, size_if_big, size_if_not, sem):
        @pl.when(big(way))
        def _():
            wait_for(size_if_big, sem)

        @pl.when(jnp.logical_not(big(way)))
        def _():
            wait_for(size_if_not, sem)

    def pass_on(phase, kind, q):
        way = course(kind, q)
        here = side_in.at[phase, kind, q]
        sem = block_recv.at[phase, kind, q]
        either(way, here.at[0:4], here.at[0:3], sem)
        sems = block_send.at[phase], fwd_recv.at[phase, kind, q]

        @pl.when(big(way))
        def _():
            remote(here.at[0:4], here.at[4:8], *sems, beside_me)

        @pl.when(jnp.logical_not(big(way)))
        def _():
            remote(here.at[0:2], here.at[4:6], *sems, beside_me)

    def weight(k, r, i):
        both = [row_weight(2 * at + r - i) for at in k]
        return both[0] if both[0] == both[1] else jnp.where(core == 0, both[0], both[1])

    def weighed(terms):
        outs = [None, None]
        for k, rows in terms:
            for r in range(2):
                for i in range(2):
                    if any(row_weight(2 * at + r - i) for at in k):
                        term = rows[r] * weight(k, r, i)
                        outs[i] = term if outs[i] is None else outs[i] + term
        return outs

    def halves(field):
        return [field[:piece], field[piece:]]

    def far_row(phase, kind, q):
        way = course(kind, q)
        at = 2 + jnp.where(big(way), 1 if way > 0 else 0, 0)
        value = side_in[phase, kind, q, at].astype(F32) * row_weight(7)
        return value, 0 if way > 0 else 1

    def from_side(phase, kind, q, extra=()):
        way = course(kind, q)
        here = side_in.at[phase, kind, q]
        either(way, here.at[4:6], here.at[4:8], fwd_recv.at[phase, kind, q])
        rows = [here[k].astype(F32) for k in (0, 1, 4, 5)]
        rows += [jnp.where(big(way), 0.0, here[k].astype(F32)) for k in (6, 7)]
        outs = weighed(
            [
                ((-2 * way,) * 2, rows[0:2]),
                ((1 - 2 * way, -1 - 2 * way), rows[2:4]),
                ((-3 * way,) * 2, rows[4:6]),
                *extra,
            ]
        )
        value, i = far_row(phase, kind, q)
        outs[i] = outs[i] + value
        return jnp.concatenate(outs, axis=0)

    strip_rows = 2 * piece * STRIP // cols
    lane = lax.broadcasted_iota(jnp.int32, (strip_rows, cols), 1)

    def send_strips(phase, kind, q, field):
        last = first = jnp.zeros((strip_rows, cols), F32)
        for j in range(cols // STRIP):
            group = field[j * strip_rows : (j + 1) * strip_rows]
            mine = lane // STRIP == j
            last = jnp.where(mine, pltpu.roll(group, ((j + 1) * STRIP) % cols, 1), last)
            first = jnp.where(mine, pltpu.roll(group, j * STRIP, 1), first)
        for side, strip in enumerate((last, first)):
            strip_out[phase, kind, q, side] = strip.astype(BF16)
            remote(
                strip_out.at[phase, kind, q, side],
                strip_in.at[phase, kind, q, side],
                strip_send.at[phase],
                strip_recv.at[phase, kind, q],
                col_block(1 - 2 * side),
            )

    def filter_cols(phase, kind, q, field):
        wait_for(strip_in.at[phase, kind, q], strip_recv.at[phase, kind, q])
        left = strip_in[phase, kind, q, 0].astype(F32)
        right = strip_in[phase, kind, q, 1].astype(F32)
        strips = []
        for j in range(cols // STRIP):
            strips.append(
                jnp.where(
                    lane < cols // 2,
                    pltpu.roll(right, (cols - j * STRIP) % cols, 1),
                    pltpu.roll(left, cols - (j + 1) * STRIP, 1),
                )
            )
        strips = jnp.concatenate(strips, axis=0).astype(BF16)
        high = field.astype(BF16)
        low = (field - high.astype(F32)).astype(BF16)
        return jnp.dot(
            jnp.concatenate([high, high, strips, strips, low], axis=1),
            wcol[...],
            preferred_element_type=F32,
        )

    def form_sources(phase, q, grid):
        value = [grid[x * levels : (x + 1) * levels] for x in range(2)]
        mean = [average[x * levels : (x + 1) * levels] for x in range(2)]

        def one(i, carry):
            m = q * piece + i
            for x in range(2):
                if phase == 0:
                    anomaly = ((arch[m, x].astype(F32) - mean[x]) * scale).astype(BF16)
                    arch[m, x] = anomaly
                else:
                    anomaly = arch[m, x]
                product = anomaly.astype(F32) * value[x]
                part[x, pl.ds(pl.multiple_of(i * 8, 8), 8), :] = (
                    product[0:8] + product[8:16]
                ) + (product[16:24] + product[24:32])
            return carry

        lax.fori_loop(0, piece, one, 0, unroll=4)
        for x in range(2):
            for g in range(piece // 8):
                rows = [part[x, pl.ds(g * 64 + k, 8, stride=8), :] for k in range(8)]
                s_ref[q, x * piece + g * 8 : x * piece + g * 8 + 8, :] = (
                    (rows[0] + rows[1]) + (rows[2] + rows[3])
                ) + ((rows[4] + rows[5]) + (rows[6] + rows[7]))

    def member_sum(pieces, carry):
        def one(i, carry):
            for q in pieces:
                carry = tuple(
                    carry[x]
                    + arch[q * piece + i, x].astype(F32) * t_ref[q, pl.ds(x * piece + i, 1), :]
                    for x in range(2)
                )
            return carry

        return lax.fori_loop(0, piece, one, carry, unroll=4)

    def spread(phase, grid, meanwhile, half_in, near_end):
        for q in ORDER:
            form_sources(phase, q, grid)
            send_strips(phase, SOURCE, q, s_ref[q])
            send_block(phase, SOURCE, q, s_ref[q])
        meanwhile()
        for q in ORDER:
            h_ref[phase, q] = filter_cols(phase, SOURCE, q, s_ref[q])
            send_block(phase, FILTERED, q, h_ref[phase, q])
            remote(
                out_ref.at[phase, FILTERED, q],
                beside_in.at[phase, q],
                block_send.at[phase],
                beside_recv.at[phase, q],
                beside_me,
            )
        for q in ORDER:
            pass_on(phase, SOURCE, q)
        for q in ORDER:
            wait_for(beside_in.at[phase, q], beside_recv.at[phase, q])
        half_in()
        for q in ORDER:
            f_ref[q] = from_side(phase, SOURCE, q)
            send_strips(phase, FILTERED, q, f_ref[q])

        def finish(pieces, carry):
            for q in pieces:
                rest = from_side(
                    phase,
                    FILTERED,
                    q,
                    (
                        ((0, 0), halves(h_ref[phase, q])),
                        ((1, -1), [beside_in[phase, q, r].astype(F32) for r in range(2)]),
                    ),
                )
                t_ref[q] = filter_cols(phase, FILTERED, q, f_ref[q]) + rest
            return member_sum(pieces, carry)

        carry = tuple(jnp.zeros((levels, cols), F32) for _ in range(2))
        for q in ORDER:
            pass_on(phase, FILTERED, q)
        carry = finish(ORDER[:2], carry)
        near_end()
        carry = finish(ORDER[2:], carry)
        for x in range(2):
            for h in range(2):
                pmine[phase, h, x] = carry[x][h * half : (h + 1) * half]
        return jnp.concatenate(carry, axis=0)

    def dotted(phase, factor):
        total = None
        for q in ORDER:
            way = course(SOURCE, q)
            here = side_in.at[phase, SOURCE, q]
            own = halves(s_ref[q])
            near = [here[r].astype(F32) * 2.0 for r in range(2)]
            far = [jnp.where(big(way), here[2 + r].astype(F32) * 2.0, 0.0) for r in range(2)]
            mine = weighed([((0, 0), own), ((-2 * way,) * 2, near)])
            value, i = far_row(phase, SOURCE, q)
            mine[i] = mine[i] + value * 2.0
            theirs = weighed(
                [
                    ((-1, 1), own),
                    ((-2 * way - 1, -2 * way + 1), near),
                    ((-3 * way,) * 2, far),
                ]
            )
            field = halves(h_ref[phase, q])
            for i in range(2):
                beside = beside_in[phase, q, i].astype(F32)
                if factor is None:
                    term = mine[i] * field[i] + theirs[i] * beside
                else:
                    term = (mine[i] * factor) * (field[i] * factor) + (theirs[i] * factor) * (
                        beside * factor
                    )
                total = term if total is None else total + term
        return jnp.sum(total, axis=0, keepdims=True)

    def send_increment(phase):
        return remote(
            pmine.at[phase, other], ptheirs.at[phase], p_sem.at[2], p_sem.at[phase], partner
        )

    def folded(vector):
        return (
            sum(vector[:, k * cols : (k + 1) * cols] for k in range(n_obs // cols)) * 0.5
        )

    def reduce_first(which, rows):
        red1[which, gx, 0:1, :] = rows[0]
        red1[which, gx, 1:2, :] = rows[1]
        mine = red1.at[which, gx]
        for k in range(1, n_gx):
            remote(mine, mine, red_send.at[which, 0], red_recv.at[which, 0], row_block(k))

    def reduce_second(which):
        wait_for(red1.at[which, 0 : n_gx - 1], red_recv.at[which, 0])
        red2[which, plane] = jnp.sum(red1[which], axis=0)
        mine = red2.at[which, plane]
        for k in range(1, n_plane):
            remote(mine, mine, red_send.at[which, 1], red_recv.at[which, 1], plane_device(k))

    def reduce_last(which):
        wait_for(red2.at[which, 0 : n_plane - 1], red_recv.at[which, 1])
        both = jnp.sum(jnp.sum(red2[which], axis=0), axis=1, keepdims=True)
        return both[0:1], both[1:2]

    def nothing():
        pass

    grid_b = spread(0, scatter(innovation), nothing, nothing, nothing)
    gsum[ma] = gather(grid_b)
    g_copy = remote(gsum.at[ma], gsum.at[ma], g_sem.at[0], g_sem.at[1], partner)
    send_increment(0)
    reduce_first(
        0,
        (
            folded(innovation * innovation),
            dotted(0, None) + folded(noise * innovation * innovation),
        ),
    )
    g_copy.wait()
    image = gsum[0] + gsum[1] + noise * innovation

    state = {}

    def meanwhile():
        reduce_second(0)

    def half_in():
        norm_now, product = reduce_last(0)
        alpha = norm_now / product
        scaled = alpha * image
        residual = innovation - scaled
        change = folded(scaled * (noise * scaled - 2.0 * image))
        reduce_first(1, (folded(residual * residual), dotted(1, alpha) + change))
        state["step"] = norm_now, product, alpha, residual

    def near_end():
        reduce_second(1)

    spread(1, scatter(image), meanwhile, half_in, near_end)
    send_increment(1)
    for phase in range(2):
        wait_for(sent_rows, block_send.at[phase])
        wait_for(strip_in.at[phase], strip_send.at[phase])
        wait_for(red1.at[phase, 0 : n_gx - 1], red_send.at[phase, 0])
    wait_for(red2.at[0, 0 : n_plane - 1], red_send.at[0, 1])
    wait_for(ptheirs.at[0], p_sem.at[0])

    norm_now, product, alpha, residual = state["step"]
    norm_next, change = reduce_last(1)
    product = product + change
    ratio = norm_next / norm_now
    alpha_next = norm_next / (product - ratio * norm_next / alpha)
    weights = alpha * innovation + alpha_next * (residual + ratio * innovation)
    chosen = jnp.where(ma == 0, weights[:, : n_obs // 2], weights[:, n_obs // 2 :])
    w_ref[0:1, :] = chosen[:, :cols]
    w_ref[1:2, :] = chosen[:, cols:]

    wait_for(ptheirs.at[1], p_sem.at[1])
    first_weight = (alpha + alpha_next * (1.0 + ratio))[None]
    second_weight = (alpha * alpha_next)[None]
    inc_ref[...] = first_weight * (pmine[0, ma] + ptheirs[0]) - second_weight * (
        pmine[1, ma] + ptheirs[1]
    )

    wait_for(ptheirs, p_sem.at[2])
    wait_for(red2.at[1, 0 : n_plane - 1], red_send.at[1, 1])


def shards(n_gx, n_gy, archive, obs_index, obs_value, obs_error):
    members, rows, levels, cols = archive.shape
    half = levels // 2
    n_own = obs_index.shape[0]
    piece = members // CHUNKS
    strip_rows = rows * piece * STRIP // cols
    shape = (n_own // cols, cols)
    dma = pltpu.SemaphoreType.DMA
    vmem = pl.BlockSpec(memory_space=pltpu.VMEM)
    hbm = pl.BlockSpec(memory_space=pltpu.HBM)
    increment, weights = pl.pallas_call(
        functools.partial(kernel, n_gx, n_gy),
        out_shape=(
            pltpu.VMEM((rows, half, cols), F32),
            pltpu.VMEM(shape, F32),
        ),
        in_specs=[hbm, hbm, hbm, hbm],
        out_specs=(vmem, vmem),
        scratch_shapes=[
            pltpu.VMEM((members, rows, levels, cols), BF16),
            pltpu.VMEM(shape, jnp.int32),
            pltpu.VMEM((2, *shape), F32),
            pltpu.VMEM((2, 8, cols), F32),
            pltpu.VMEM((2, rows * levels, cols), F32),
            pltpu.VMEM((rows, piece * 8, cols), F32),
            pltpu.VMEM((CHUNKS, rows * piece, cols), F32),
            pltpu.VMEM((CHUNKS, rows * piece, cols), F32),
            pltpu.VMEM((2, CHUNKS, rows * piece, cols), F32),
            pltpu.VMEM((CHUNKS, rows * piece, cols), F32),
            pltpu.VMEM((2, 2, CHUNKS, rows, piece, cols), BF16),
            pltpu.VMEM((2, 2, CHUNKS, 8, piece, cols), BF16),
            pltpu.VMEM((2, CHUNKS, rows, piece, cols), BF16),
            pltpu.VMEM((15 * CHUNKS, piece, cols), BF16),
            pltpu.VMEM((2, 2, CHUNKS, 2, strip_rows, cols), BF16),
            pltpu.VMEM((2, 2, CHUNKS, 2, strip_rows, cols), BF16),
            pltpu.VMEM((5 * cols, cols), BF16),
            pltpu.VMEM((2, 2, rows, half, cols), F32),
            pltpu.VMEM((2, rows, half, cols), F32),
            pltpu.VMEM((2, 1, 2 * n_own), F32),
            pltpu.VMEM((2, n_gx, 2, cols), F32),
            pltpu.VMEM((2, 2 * n_gy, 2, cols), F32),
            dma((LOADS + 2,)),
            dma((2,)),
            dma((2,)),
            dma((2,)),
            dma((2, 2, CHUNKS)),
            dma((2, 2, CHUNKS)),
            dma((2, CHUNKS)),
            dma((2,)),
            dma((2, 2, CHUNKS)),
            dma((3,)),
            dma((2,)),
            dma((2, 2)),
            dma((2, 2)),
        ],
        compiler_params=pltpu.CompilerParams(
            collective_id=0, has_side_effects=True, vmem_limit_bytes=56 * 1024 * 1024
        ),
        name="analysis",
    )(archive, obs_index.reshape(shape), obs_value.reshape(shape), obs_error.reshape(shape))
    return increment, weights.reshape(n_own)


def solution(mesh):
    n_gx, n_gy = mesh.shape["gx"], mesh.shape["gy"]
    own = P(("gx", "gy", "ma"))
    return jax.shard_map(
        functools.partial(shards, n_gx, n_gy),
        mesh=mesh,
        in_specs=(P("ma", "gx", None, "gy"), own, own, own),
        out_specs=(P("gx", "ma", "gy"), own),
        check_vma=False,
    )
```

time: 61 us -> 51.4 us (0.84)
  Pallas kernels: 57.7 us -> 49.5 us
  local copies, waits for them, and re-layouts: 2.54 us -> 1.17 us
    pallas_call x1, Pallas kernels: 57.7 us -> 49.5 us  [shards(): pl.pallas_call(functools.partial(kernel, n_gx, n_gy), out_shape=(pltpu.VM...]
    unnamed x2, local copies, waits for them, and re-layouts: 2.54 us -> 1.17 us
where the time goes in v3:
time: 51.4 us; the launch traced here: 51.3 us
  Pallas kernels  49.5 us (96%)
  local copies, waits for them, and re-layouts  1.17 us (2%)
  between operations  0.64 us (1%)
    pallas_call x1, Pallas kernels, shards(): pl.pallas_call(functools.partial(kernel, n_gx, n_gy), out_shape=(pltpu.VM...  49.5 us
    unnamed x2, local copies, waits for them, and re-layouts  1.17 us

profile of v3, /device:TPU:1, one launch (start us, length us, event | category | flops | bytes accessed | tf_op | source)
XLA Modules:
  0.0 51.3 jit_solution(8182527985117461808)
XLA Ops:
  0.6 49.5 %analysis.1 = (f32[2,16,128]{2,1,0:T(8,128)S(1)}, f32[2,128]{1,0:T(2,128)S(1)}) custom-call(bf16[256,2,32,128]{3,2,1,0:T(8,128)(2,1)} %archive_hbm.1, s32[2,128]{1,0:T(2,128)} %bitcast.5, f32[2,128]{1,0:T(2,128)} %bitcast.6, f32[2,128]{1,0:T(2,128)} %bitcast.7), custom_call_target="tpu_custom_call" | custom-call | tf_op jit(solution)/shard_map/analysis/pallas_call | solution.py:600
  50.1 0.6 %copy.8 = f32[2,16,128]{2,1,0:T(8,128)} copy(f32[2,16,128]{2,1,0:T(8,128)S(1)} %get-tuple-element.6) | data formatting | bytes 32768
  50.7 0.6 %copy.9 = f32[256]{0:T(256)} copy(f32[256]{0:T(256)S(1)} %bitcast.4) | data formatting | bytes 2048

commit v4 on v3

--- a/solution.py
+++ b/solution.py
@@ -94,6 +94,7 @@
     gsum,
     red1,
     red2,
+    count_ref,
     load_sem,
     meta_sem,
     sums_sem,
@@ -164,6 +165,8 @@
         pl.semaphore_signal(barrier, inc=1, device_id=row_block(k), device_id_type=MESH)
     for k in range(1, n_plane):
         pl.semaphore_signal(barrier, inc=1, device_id=plane_device(k), device_id_type=MESH)
+        across = {**plane_device(k), **row_block(1 - 2 * core)}
+        pl.semaphore_signal(barrier, inc=1, device_id=across, device_id_type=MESH)
 
     source = lax.broadcasted_iota(jnp.int32, (cols, cols), 0)
     target = lax.broadcasted_iota(jnp.int32, (cols, cols), 1)
@@ -199,7 +202,7 @@
     meta[ma, 4:6, :] = pair_ref[1]
     meta[ma, 6:8, :] = jnp.zeros((2, cols), F32)
 
-    pl.semaphore_wait(barrier, n_gx - 1 + n_plane - 1)
+    pl.semaphore_wait(barrier, n_gx - 1 + 2 * (n_plane - 1))
 
     partner = {"ma": other}
     meta_copy = remote(meta.at[ma], meta.at[ma], meta_sem.at[0], meta_sem.at[1], partner)
@@ -316,10 +319,13 @@
         value = side_in[phase, kind, q, at].astype(F32) * row_weight(7)
         return value, 0 if way > 0 else 1
 
+    def passed_in(phase, kind, q):
+        here = side_in.at[phase, kind, q]
+        either(course(kind, q), here.at[4:6], here.at[4:8], fwd_recv.at[phase, kind, q])
+
     def from_side(phase, kind, q, extra=()):
         way = course(kind, q)
         here = side_in.at[phase, kind, q]
-        either(way, here.at[4:6], here.at[4:8], fwd_recv.at[phase, kind, q])
         rows = [here[k].astype(F32) for k in (0, 1, 4, 5)]
         rows += [jnp.where(big(way), 0.0, here[k].astype(F32)) for k in (6, 7)]
         outs = weighed(
@@ -354,8 +360,10 @@
                 col_block(1 - 2 * side),
             )
 
+    def strips_in(phase, kind, q):
+        wait_for(strip_in.at[phase, kind, q], strip_recv.at[phase, kind, q])
+
     def filter_cols(phase, kind, q, field):
-        wait_for(strip_in.at[phase, kind, q], strip_recv.at[phase, kind, q])
         left = strip_in[phase, kind, q, 0].astype(F32)
         right = strip_in[phase, kind, q, 1].astype(F32)
         strips = []
@@ -394,7 +402,7 @@
                 ) + (product[16:24] + product[24:32])
             return carry
 
-        lax.fori_loop(0, piece, one, 0, unroll=4)
+        lax.fori_loop(0, piece, one, 0, unroll=8)
         for x in range(2):
             for g in range(piece // 8):
                 rows = [part[x, pl.ds(g * 64 + k, 8, stride=8), :] for k in range(8)]
@@ -412,35 +420,60 @@
                 )
             return carry
 
-        return lax.fori_loop(0, piece, one, carry, unroll=4)
-
-    def spread(phase, grid, meanwhile, half_in, near_end):
+        return lax.fori_loop(0, piece, one, carry, unroll=8)
+
+    def spread(phase, grid, before_last, half_in, near_end):
         for q in ORDER:
             form_sources(phase, q, grid)
             send_strips(phase, SOURCE, q, s_ref[q])
             send_block(phase, SOURCE, q, s_ref[q])
-        meanwhile()
-        for q in ORDER:
-            h_ref[phase, q] = filter_cols(phase, SOURCE, q, s_ref[q])
-            send_block(phase, FILTERED, q, h_ref[phase, q])
-            remote(
-                out_ref.at[phase, FILTERED, q],
-                beside_in.at[phase, q],
-                block_send.at[phase],
-                beside_recv.at[phase, q],
-                beside_me,
-            )
-        for q in ORDER:
-            pass_on(phase, SOURCE, q)
+        def filter_own(pieces):
+            for q in pieces:
+                strips_in(phase, SOURCE, q)
+                h_ref[phase, q] = filter_cols(phase, SOURCE, q, s_ref[q])
+                send_block(phase, FILTERED, q, h_ref[phase, q])
+                remote(
+                    out_ref.at[phase, FILTERED, q],
+                    beside_in.at[phase, q],
+                    block_send.at[phase],
+                    beside_recv.at[phase, q],
+                    beside_me,
+                )
+
+        def filter_one_side(pieces):
+            for q in pieces:
+                passed_in(phase, SOURCE, q)
+                f_ref[q] = from_side(phase, SOURCE, q)
+                send_strips(phase, FILTERED, q, f_ref[q])
+
+        early, late = ORDER[:2], ORDER[2:]
+        filter_own(early)
+        if phase == 0:
+            for q in early:
+                pass_on(phase, SOURCE, q)
+            filter_own(late[:1])
+            filter_one_side(early)
+            filter_own(late[1:])
+        else:
+            filter_own(late)
+            for q in early:
+                pass_on(phase, SOURCE, q)
         for q in ORDER:
             wait_for(beside_in.at[phase, q], beside_recv.at[phase, q])
+        before_last()
+        for q in late:
+            pass_on(phase, SOURCE, q)
         half_in()
-        for q in ORDER:
-            f_ref[q] = from_side(phase, SOURCE, q)
-            send_strips(phase, FILTERED, q, f_ref[q])
+        if phase == 1:
+            filter_one_side(early)
+        filter_one_side(late)
 
         def finish(pieces, carry):
             for q in pieces:
+                passed_in(phase, FILTERED, q)
+                strips_in(phase, FILTERED, q)
+            filtered = [filter_cols(phase, FILTERED, q, f_ref[q]) for q in pieces]
+            for q, of_one_side in zip(pieces, filtered):
                 rest = from_side(
                     phase,
                     FILTERED,
@@ -450,23 +483,29 @@
                         ((1, -1), [beside_in[phase, q, r].astype(F32) for r in range(2)]),
                     ),
                 )
-                t_ref[q] = filter_cols(phase, FILTERED, q, f_ref[q]) + rest
+                t_ref[q] = of_one_side + rest
             return member_sum(pieces, carry)
 
         carry = tuple(jnp.zeros((levels, cols), F32) for _ in range(2))
-        for q in ORDER:
-            pass_on(phase, FILTERED, q)
-        carry = finish(ORDER[:2], carry)
-        near_end()
-        carry = finish(ORDER[2:], carry)
+        if phase == 0:
+            for pieces in (early, late):
+                for q in pieces:
+                    pass_on(phase, FILTERED, q)
+                carry = finish(pieces, carry)
+        else:
+            for q in ORDER:
+                pass_on(phase, FILTERED, q)
+            carry = finish(early, carry)
+            near_end()
+            carry = finish(late, carry)
         for x in range(2):
             for h in range(2):
                 pmine[phase, h, x] = carry[x][h * half : (h + 1) * half]
         return jnp.concatenate(carry, axis=0)
 
-    def dotted(phase, factor):
+    def dotted(phase, factor, pieces):
         total = None
-        for q in ORDER:
+        for q in pieces:
             way = course(SOURCE, q)
             here = side_in.at[phase, SOURCE, q]
             own = halves(s_ref[q])
@@ -504,66 +543,89 @@
             sum(vector[:, k * cols : (k + 1) * cols] for k in range(n_obs // cols)) * 0.5
         )
 
+    n_z = n_gx // 2
+    hub = core == 1
+
     def reduce_first(which, rows):
         red1[which, gx, 0:1, :] = rows[0]
         red1[which, gx, 1:2, :] = rows[1]
         mine = red1.at[which, gx]
-        for k in range(1, n_gx):
-            remote(mine, mine, red_send.at[which, 0], red_recv.at[which, 0], row_block(k))
+        sems = red_send.at[which, 0], red_recv.at[which, 0]
+        for k in range(1, n_z):
+            remote(mine, mine, *sems, {"gx": 2 * lax.rem(gx // 2 + k, n_z) + 1})
+
+        @pl.when(jnp.logical_not(hub))
+        def _():
+            remote(mine, mine, *sems, {"gx": gx + 1})
 
     def reduce_second(which):
-        wait_for(red1.at[which, 0 : n_gx - 1], red_recv.at[which, 0])
-        red2[which, plane] = jnp.sum(red1[which], axis=0)
-        mine = red2.at[which, plane]
-        for k in range(1, n_plane):
-            remote(mine, mine, red_send.at[which, 1], red_recv.at[which, 1], plane_device(k))
+        @pl.when(hub)
+        def _():
+            wait_for(red1.at[which, 0 : n_gx - 1], red_recv.at[which, 0])
+            red2[which, plane] = jnp.sum(red1[which], axis=0)
+            mine = red2.at[which, plane]
+            sems = red_send.at[which, 1], red_recv.at[which, 1]
+            for k in range(1, n_plane):
+                remote(mine, mine, *sems, {**plane_device(k), "gx": gx - 1})
+            for k in range(1, n_plane):
+                remote(mine, mine, *sems, plane_device(k))
+            remote(mine, mine, *sems, {"gx": gx - 1})
 
     def reduce_last(which):
-        wait_for(red2.at[which, 0 : n_plane - 1], red_recv.at[which, 1])
+        @pl.when(hub)
+        def _():
+            wait_for(red2.at[which, 0 : n_plane - 1], red_recv.at[which, 1])
+
+        @pl.when(jnp.logical_not(hub))
+        def _():
+            wait_for(red2.at[which, 0:n_plane], red_recv.at[which, 1])
+
         both = jnp.sum(jnp.sum(red2[which], axis=0), axis=1, keepdims=True)
         return both[0:1], both[1:2]
 
-    def nothing():
-        pass
-
-    grid_b = spread(0, scatter(innovation), nothing, nothing, nothing)
+    def reduce_sent(which):
+        @pl.when(hub)
+        def _():
+            wait_for(count_ref.at[0 : n_z - 1], red_send.at[which, 0])
+            wait_for(count_ref.at[0 : 2 * n_plane - 1], red_send.at[which, 1])
+
+        @pl.when(jnp.logical_not(hub))
+        def _():
+            wait_for(count_ref.at[0:n_z], red_send.at[which, 0])
+
+    def first_half_in():
+        product = folded(noise * innovation * innovation) + dotted(0, None, ORDER)
+        reduce_first(0, (folded(innovation * innovation), product))
+
+    grid_b = spread(0, scatter(innovation), lambda: None, first_half_in, lambda: None)
     gsum[ma] = gather(grid_b)
     g_copy = remote(gsum.at[ma], gsum.at[ma], g_sem.at[0], g_sem.at[1], partner)
     send_increment(0)
-    reduce_first(
-        0,
-        (
-            folded(innovation * innovation),
-            dotted(0, None) + folded(noise * innovation * innovation),
-        ),
-    )
+    reduce_second(0)
     g_copy.wait()
     image = gsum[0] + gsum[1] + noise * innovation
 
     state = {}
 
-    def meanwhile():
-        reduce_second(0)
-
-    def half_in():
+    def before_last():
         norm_now, product = reduce_last(0)
         alpha = norm_now / product
         scaled = alpha * image
         residual = innovation - scaled
-        change = folded(scaled * (noise * scaled - 2.0 * image))
-        reduce_first(1, (folded(residual * residual), dotted(1, alpha) + change))
+        change = folded(scaled * (noise * scaled - 2.0 * image)) + dotted(1, alpha, ORDER[:2])
         state["step"] = norm_now, product, alpha, residual
-
-    def near_end():
-        reduce_second(1)
-
-    spread(1, scatter(image), meanwhile, half_in, near_end)
+        state["sums"] = folded(residual * residual), change
+
+    def half_in():
+        norm, change = state["sums"]
+        reduce_first(1, (norm, change + dotted(1, state["step"][2], ORDER[2:])))
+
+    spread(1, scatter(image), before_last, half_in, lambda: reduce_second(1))
     send_increment(1)
     for phase in range(2):
         wait_for(sent_rows, block_send.at[phase])
         wait_for(strip_in.at[phase], strip_send.at[phase])
-        wait_for(red1.at[phase, 0 : n_gx - 1], red_send.at[phase, 0])
-    wait_for(red2.at[0, 0 : n_plane - 1], red_send.at[0, 1])
+    reduce_sent(0)
     wait_for(ptheirs.at[0], p_sem.at[0])
 
     norm_now, product, alpha, residual = state["step"]
@@ -584,7 +646,7 @@
     )
 
     wait_for(ptheirs, p_sem.at[2])
-    wait_for(red2.at[1, 0 : n_plane - 1], red_send.at[1, 1])
+    reduce_sent(1)
 
 
 def shards(n_gx, n_gy, archive, obs_index, obs_value, obs_error):
@@ -628,6 +690,7 @@
             pltpu.VMEM((2, 1, 2 * n_own), F32),
             pltpu.VMEM((2, n_gx, 2, cols), F32),
             pltpu.VMEM((2, 2 * n_gy, 2, cols), F32),
+            pltpu.VMEM((4 * n_gy, 2, cols), F32),
             dma((LOADS + 2,)),
             dma((2,)),
             dma((2,)),

time: 51.4 us -> 50.7 us (0.986)
  Pallas kernels: 49.5 us -> 48.8 us
    pallas_call x1, Pallas kernels: 49.5 us -> 48.8 us  [shards(): pl.pallas_call(functools.partial(kernel, n_gx, n_gy), out_shape=(pltpu.VM...]
where the time goes in v4:
time: 50.7 us; the launch traced here: 50.6 us
  Pallas kernels  48.8 us (96%)
  local copies, waits for them, and re-layouts  1.17 us (2%)
  between operations  0.64 us (1%)
    pallas_call x1, Pallas kernels, shards(): pl.pallas_call(functools.partial(kernel, n_gx, n_gy), out_shape=(pltpu.VM...  48.8 us
    unnamed x2, local copies, waits for them, and re-layouts  1.17 us

profile of v4, /device:TPU:1, one launch (start us, length us, event | category | flops | bytes accessed | tf_op | source)
XLA Modules:
  0.0 50.6 jit_solution(3115626673809752508)
XLA Ops:
  0.6 48.8 %analysis.1 = (f32[2,16,128]{2,1,0:T(8,128)S(1)}, f32[2,128]{1,0:T(2,128)S(1)}) custom-call(bf16[256,2,32,128]{3,2,1,0:T(8,128)(2,1)} %archive_hbm.1, s32[2,128]{1,0:T(2,128)} %bitcast.5, f32[2,128]{1,0:T(2,128)} %bitcast.6, f32[2,128]{1,0:T(2,128)} %bitcast.7), custom_call_target="tpu_custom_call" | custom-call | tf_op jit(solution)/shard_map/analysis/pallas_call | solution.py:662
  49.5 0.6 %copy.8 = f32[2,16,128]{2,1,0:T(8,128)} copy(f32[2,16,128]{2,1,0:T(8,128)S(1)} %get-tuple-element.6) | data formatting | bytes 32768
  50.1 0.6 %copy.9 = f32[256]{0:T(256)} copy(f32[256]{0:T(256)S(1)} %bitcast.4) | data formatting | bytes 2048

commit v5 on v4

--- a/solution.py
+++ b/solution.py
@@ -17,13 +17,13 @@
 
 LOADS = 8
 CHUNKS = 4
-ORDER = (0, 2, 1, 3)
+PAIRS = CHUNKS // 2
 STRIP = 16
 SOURCE, FILTERED = 0, 1
 
 
 def course(kind, q):
-    return (1 if q < CHUNKS // 2 else -1) * (1 if kind == SOURCE else -1)
+    return (1 if q % 2 == 0 else -1) * (1 if kind == SOURCE else -1)
 
 
 def row_weight(distance):
@@ -85,7 +85,7 @@
     out_ref,
     side_in,
     beside_in,
-    sent_ref,
+    count_rows,
     strip_out,
     strip_in,
     wcol,
@@ -119,7 +119,7 @@
     ma = lax.axis_index("ma")
     core = lax.rem(gx, 2)
     other = 1 - ma
-    sent_rows = sent_ref.at[0 : 15 * CHUNKS]
+    sent_rows = count_rows.at[0 : 15 * CHUNKS]
     plane = gy * 2 + ma
     n_plane = n_gy * 2
 
@@ -161,12 +161,38 @@
     pltpu.make_async_copy(err_hbm, pair_ref.at[1], load_sem.at[LOADS + 1]).start()
 
     barrier = pltpu.get_barrier_semaphore()
-    for k in range(1, n_gx):
+    def far_first(count):
+        return sorted(range(1, count), key=lambda k: -min(k, count - k))
+
+    for k in far_first(n_gx):
         pl.semaphore_signal(barrier, inc=1, device_id=row_block(k), device_id_type=MESH)
-    for k in range(1, n_plane):
-        pl.semaphore_signal(barrier, inc=1, device_id=plane_device(k), device_id_type=MESH)
+    for k in far_first(n_plane):
         across = {**plane_device(k), **row_block(1 - 2 * core)}
-        pl.semaphore_signal(barrier, inc=1, device_id=across, device_id_type=MESH)
+        for device in (plane_device(k), across):
+            pl.semaphore_signal(barrier, inc=1, device_id=device, device_id_type=MESH)
+
+    total = tuple(jnp.zeros((levels, cols), F32) for _ in range(2))
+    for k in range(LOADS):
+        loads[k].wait()
+
+        def add(m, carry):
+            return tuple(carry[x] + arch[m, x].astype(F32) for x in range(2))
+
+        total = lax.fori_loop(k * load, (k + 1) * load, add, total, unroll=8)
+    for x in range(2):
+        sums[ma, x * levels : (x + 1) * levels, :] = total[x]
+    wait_for(idx_ref, load_sem.at[LOADS])
+    wait_for(pair_ref, load_sem.at[LOADS + 1])
+    meta[ma, 0:2, :] = idx_ref[...].astype(F32)
+    meta[ma, 2:4, :] = pair_ref[0]
+    meta[ma, 4:6, :] = pair_ref[1]
+    meta[ma, 6:8, :] = jnp.zeros((2, cols), F32)
+
+    pl.semaphore_wait(barrier, n_gx - 1 + 2 * (n_plane - 1))
+
+    partner = {"ma": other}
+    meta_copy = remote(meta.at[ma], meta.at[ma], meta_sem.at[0], meta_sem.at[1], partner)
+    sums_copy = remote(sums.at[ma], sums.at[ma], sums_sem.at[0], sums_sem.at[1], partner)
 
     source = lax.broadcasted_iota(jnp.int32, (cols, cols), 0)
     target = lax.broadcasted_iota(jnp.int32, (cols, cols), 1)
@@ -184,29 +210,6 @@
         wcol[(2 * k + 1) * cols : (2 * k + 2) * cols, :] = low
         if k == 0:
             wcol[4 * cols : 5 * cols, :] = high
-
-    total = tuple(jnp.zeros((levels, cols), F32) for _ in range(2))
-    for k in range(LOADS):
-        loads[k].wait()
-
-        def add(m, carry):
-            return tuple(carry[x] + arch[m, x].astype(F32) for x in range(2))
-
-        total = lax.fori_loop(k * load, (k + 1) * load, add, total, unroll=8)
-    for x in range(2):
-        sums[ma, x * levels : (x + 1) * levels, :] = total[x]
-    wait_for(idx_ref, load_sem.at[LOADS])
-    wait_for(pair_ref, load_sem.at[LOADS + 1])
-    meta[ma, 0:2, :] = idx_ref[...].astype(F32)
-    meta[ma, 2:4, :] = pair_ref[0]
-    meta[ma, 4:6, :] = pair_ref[1]
-    meta[ma, 6:8, :] = jnp.zeros((2, cols), F32)
-
-    pl.semaphore_wait(barrier, n_gx - 1 + 2 * (n_plane - 1))
-
-    partner = {"ma": other}
-    meta_copy = remote(meta.at[ma], meta.at[ma], meta_sem.at[0], meta_sem.at[1], partner)
-    sums_copy = remote(sums.at[ma], sums.at[ma], sums_sem.at[0], sums_sem.at[1], partner)
 
     meta_copy.wait()
 
@@ -260,7 +263,7 @@
             out_ref[phase, kind, q, x] = field[x * piece : (x + 1) * piece].astype(BF16)
         block = out_ref.at[phase, kind, q]
         here = side_in.at[phase, kind, q]
-        sems = block_send.at[phase], block_recv.at[phase, kind, q]
+        sems = block_send.at[phase], block_recv.at[phase, kind, q // 2]
 
         @pl.when(big(way))
         def _():
@@ -272,29 +275,28 @@
 
         remote(block, here.at[0:2], *sems, row_block(2 * way))
 
-    def either(way, size_if_big, size_if_not, sem):
-        @pl.when(big(way))
-        def _():
-            wait_for(size_if_big, sem)
-
-        @pl.when(jnp.logical_not(big(way)))
-        def _():
-            wait_for(size_if_not, sem)
-
-    def pass_on(phase, kind, q):
-        way = course(kind, q)
-        here = side_in.at[phase, kind, q]
-        sem = block_recv.at[phase, kind, q]
-        either(way, here.at[0:4], here.at[0:3], sem)
-        sems = block_send.at[phase], fwd_recv.at[phase, kind, q]
-
-        @pl.when(big(way))
-        def _():
-            remote(here.at[0:4], here.at[4:8], *sems, beside_me)
-
-        @pl.when(jnp.logical_not(big(way)))
-        def _():
-            remote(here.at[0:2], here.at[4:6], *sems, beside_me)
+    def pass_on(phase, kind, pair):
+        wait_for(count_rows.at[0:7], block_recv.at[phase, kind, pair])
+        sems = block_send.at[phase], fwd_recv.at[phase, kind, pair]
+        for q in (2 * pair, 2 * pair + 1):
+            way = course(kind, q)
+            here = side_in.at[phase, kind, q]
+
+            @pl.when(big(way))
+            def _(here=here):
+                remote(here.at[0:4], here.at[4:8], *sems, beside_me)
+
+            @pl.when(jnp.logical_not(big(way)))
+            def _(here=here):
+                remote(here.at[0:2], here.at[4:6], *sems, beside_me)
+
+    def passed_in(phase, kind, pair):
+        wait_for(count_rows.at[0:6], fwd_recv.at[phase, kind, pair])
+
+    def come_beside(phase):
+        for pair in range(PAIRS):
+            both = beside_in.at[phase, 2 * pair : 2 * pair + 2]
+            wait_for(both, beside_recv.at[phase, pair])
 
     def weight(k, r, i):
         both = [row_weight(2 * at + r - i) for at in k]
@@ -318,10 +320,6 @@
         at = 2 + jnp.where(big(way), 1 if way > 0 else 0, 0)
         value = side_in[phase, kind, q, at].astype(F32) * row_weight(7)
         return value, 0 if way > 0 else 1
-
-    def passed_in(phase, kind, q):
-        here = side_in.at[phase, kind, q]
-        either(course(kind, q), here.at[4:6], here.at[4:8], fwd_recv.at[phase, kind, q])
 
     def from_side(phase, kind, q, extra=()):
         way = course(kind, q)
@@ -356,12 +354,9 @@
                 strip_out.at[phase, kind, q, side],
                 strip_in.at[phase, kind, q, side],
                 strip_send.at[phase],
-                strip_recv.at[phase, kind, q],
+                strip_recv.at[phase, q if kind == SOURCE else CHUNKS + q // 2],
                 col_block(1 - 2 * side),
             )
-
-    def strips_in(phase, kind, q):
-        wait_for(strip_in.at[phase, kind, q], strip_recv.at[phase, kind, q])
 
     def filter_cols(phase, kind, q, field):
         left = strip_in[phase, kind, q, 0].astype(F32)
@@ -423,55 +418,35 @@
         return lax.fori_loop(0, piece, one, carry, unroll=8)
 
     def spread(phase, grid, before_last, half_in, near_end):
-        for q in ORDER:
+        for q in range(CHUNKS):
             form_sources(phase, q, grid)
             send_strips(phase, SOURCE, q, s_ref[q])
             send_block(phase, SOURCE, q, s_ref[q])
-        def filter_own(pieces):
+
+        def filter_own(*pieces):
             for q in pieces:
-                strips_in(phase, SOURCE, q)
+                wait_for(strip_in.at[phase, SOURCE, q], strip_recv.at[phase, q])
                 h_ref[phase, q] = filter_cols(phase, SOURCE, q, s_ref[q])
                 send_block(phase, FILTERED, q, h_ref[phase, q])
                 remote(
                     out_ref.at[phase, FILTERED, q],
                     beside_in.at[phase, q],
                     block_send.at[phase],
-                    beside_recv.at[phase, q],
+                    beside_recv.at[phase, q // 2],
                     beside_me,
                 )
 
-        def filter_one_side(pieces):
-            for q in pieces:
-                passed_in(phase, SOURCE, q)
+        def filter_one_side(pair):
+            passed_in(phase, SOURCE, pair)
+            for q in (2 * pair, 2 * pair + 1):
                 f_ref[q] = from_side(phase, SOURCE, q)
                 send_strips(phase, FILTERED, q, f_ref[q])
 
-        early, late = ORDER[:2], ORDER[2:]
-        filter_own(early)
-        if phase == 0:
-            for q in early:
-                pass_on(phase, SOURCE, q)
-            filter_own(late[:1])
-            filter_one_side(early)
-            filter_own(late[1:])
-        else:
-            filter_own(late)
-            for q in early:
-                pass_on(phase, SOURCE, q)
-        for q in ORDER:
-            wait_for(beside_in.at[phase, q], beside_recv.at[phase, q])
-        before_last()
-        for q in late:
-            pass_on(phase, SOURCE, q)
-        half_in()
-        if phase == 1:
-            filter_one_side(early)
-        filter_one_side(late)
-
-        def finish(pieces, carry):
-            for q in pieces:
-                passed_in(phase, FILTERED, q)
-                strips_in(phase, FILTERED, q)
+        def finish(pair, carry):
+            pieces = (2 * pair, 2 * pair + 1)
+            passed_in(phase, FILTERED, pair)
+            both = strip_in.at[phase, FILTERED, pieces[0] : pieces[1] + 1]
+            wait_for(both, strip_recv.at[phase, CHUNKS + pair])
             filtered = [filter_cols(phase, FILTERED, q, f_ref[q]) for q in pieces]
             for q, of_one_side in zip(pieces, filtered):
                 rest = from_side(
@@ -486,18 +461,34 @@
                 t_ref[q] = of_one_side + rest
             return member_sum(pieces, carry)
 
+        filter_own(0, 1)
+        if phase == 0:
+            pass_on(phase, SOURCE, 0)
+            filter_own(2)
+            filter_one_side(0)
+            filter_own(3)
+        else:
+            filter_own(2, 3)
+            pass_on(phase, SOURCE, 0)
+        come_beside(phase)
+        before_last()
+        pass_on(phase, SOURCE, 1)
+        half_in()
+        if phase == 1:
+            filter_one_side(0)
+        filter_one_side(1)
+
         carry = tuple(jnp.zeros((levels, cols), F32) for _ in range(2))
         if phase == 0:
-            for pieces in (early, late):
-                for q in pieces:
-                    pass_on(phase, FILTERED, q)
-                carry = finish(pieces, carry)
+            for pair in range(PAIRS):
+                pass_on(phase, FILTERED, pair)
+                carry = finish(pair, carry)
         else:
-            for q in ORDER:
-                pass_on(phase, FILTERED, q)
-            carry = finish(early, carry)
+            for pair in range(PAIRS):
+                pass_on(phase, FILTERED, pair)
+            carry = finish(0, carry)
             near_end()
-            carry = finish(late, carry)
+            carry = finish(1, carry)
         for x in range(2):
             for h in range(2):
                 pmine[phase, h, x] = carry[x][h * half : (h + 1) * half]
@@ -594,7 +585,7 @@
             wait_for(count_ref.at[0:n_z], red_send.at[which, 0])
 
     def first_half_in():
-        product = folded(noise * innovation * innovation) + dotted(0, None, ORDER)
+        product = folded(noise * innovation * innovation) + dotted(0, None, range(CHUNKS))
         reduce_first(0, (folded(innovation * innovation), product))
 
     grid_b = spread(0, scatter(innovation), lambda: None, first_half_in, lambda: None)
@@ -612,13 +603,13 @@
         alpha = norm_now / product
         scaled = alpha * image
         residual = innovation - scaled
-        change = folded(scaled * (noise * scaled - 2.0 * image)) + dotted(1, alpha, ORDER[:2])
+        change = folded(scaled * (noise * scaled - 2.0 * image)) + dotted(1, alpha, (0, 1))
         state["step"] = norm_now, product, alpha, residual
         state["sums"] = folded(residual * residual), change
 
     def half_in():
         norm, change = state["sums"]
-        reduce_first(1, (norm, change + dotted(1, state["step"][2], ORDER[2:])))
+        reduce_first(1, (norm, change + dotted(1, state["step"][2], (2, 3))))
 
     spread(1, scatter(image), before_last, half_in, lambda: reduce_second(1))
     send_increment(1)
@@ -695,11 +686,11 @@
             dma((2,)),
             dma((2,)),
             dma((2,)),
-            dma((2, 2, CHUNKS)),
-            dma((2, 2, CHUNKS)),
-            dma((2, CHUNKS)),
+            dma((2, 2, PAIRS)),
+            dma((2, 2, PAIRS)),
+            dma((2, PAIRS)),
             dma((2,)),
-            dma((2, 2, CHUNKS)),
+            dma((2, CHUNKS + PAIRS)),
             dma((3,)),
             dma((2,)),
             dma((2, 2)),

time: 50.7 us -> 50.4 us (level)
  no operation moved by 1% of the time
where the time goes in v5:
time: 50.4 us
  Pallas kernels  48.5 us (96%)
  local copies, waits for them, and re-layouts  1.17 us (2%)
  between operations  0.64 us (1%)
    pallas_call x1, Pallas kernels, shards(): pl.pallas_call(functools.partial(kernel, n_gx, n_gy), out_shape=(pltpu.VM...  48.5 us
    unnamed x2, local copies, waits for them, and re-layouts  1.17 us

profile of v5, /device:TPU:1, one launch (start us, length us, event | category | flops | bytes accessed | tf_op | source)
XLA Modules:
  0.0 50.4 jit_solution(778428716634996587)
XLA Ops:
  0.6 48.5 %analysis.1 = (f32[2,16,128]{2,1,0:T(8,128)S(1)}, f32[2,128]{1,0:T(2,128)S(1)}) custom-call(bf16[256,2,32,128]{3,2,1,0:T(8,128)(2,1)} %archive_hbm.1, s32[2,128]{1,0:T(2,128)} %bitcast.5, f32[2,128]{1,0:T(2,128)} %bitcast.6, f32[2,128]{1,0:T(2,128)} %bitcast.7), custom_call_target="tpu_custom_call" | custom-call | tf_op jit(solution)/shard_map/analysis/pallas_call | solution.py:653
  49.2 0.6 %copy.8 = f32[2,16,128]{2,1,0:T(8,128)} copy(f32[2,16,128]{2,1,0:T(8,128)S(1)} %get-tuple-element.6) | data formatting | bytes 32768
  49.8 0.6 %copy.9 = f32[256]{0:T(256)} copy(f32[256]{0:T(256)S(1)} %bitcast.4) | data formatting | bytes 2048

commit v6 on v5

--- a/solution.py
+++ b/solution.py
@@ -77,6 +77,7 @@
     pair_ref,
     meta,
     sums,
+    average,
     part,
     s_ref,
     f_ref,
@@ -246,9 +247,12 @@
         )
         return sum_of_three(spread, rows)
 
+    values = scatter(target_value)
+    counts = lax.dot_general(
+        line_hot.astype(BF16), col_hot, (((1,), (1,)), ((), ())), preferred_element_type=F32
+    )
     sums_copy.wait()
-    average = (sums[0] + sums[1]) * (1.0 / M)
-    innovation = target_value - gather(average)
+    average[...] = (sums[0] + sums[1]) * (1.0 / M)
     scale = 1.0 / math.sqrt(M - 1.0)
 
     beside_me = row_block(1 - 2 * core)
@@ -381,13 +385,12 @@
 
     def form_sources(phase, q, grid):
         value = [grid[x * levels : (x + 1) * levels] for x in range(2)]
-        mean = [average[x * levels : (x + 1) * levels] for x in range(2)]
 
         def one(i, carry):
             m = q * piece + i
             for x in range(2):
                 if phase == 0:
-                    anomaly = ((arch[m, x].astype(F32) - mean[x]) * scale).astype(BF16)
+                    anomaly = ((arch[m, x].astype(F32) - average[x * levels : (x + 1) * levels, :]) * scale).astype(BF16)
                     arch[m, x] = anomaly
                 else:
                     anomaly = arch[m, x]
@@ -420,8 +423,11 @@
     def spread(phase, grid, before_last, half_in, near_end):
         for q in range(CHUNKS):
             form_sources(phase, q, grid)
-            send_strips(phase, SOURCE, q, s_ref[q])
+            if phase == 0:
+                send_strips(phase, SOURCE, q, s_ref[q])
             send_block(phase, SOURCE, q, s_ref[q])
+            if phase == 1:
+                send_strips(phase, SOURCE, q, s_ref[q])
 
         def filter_own(*pieces):
             for q in pieces:
@@ -444,11 +450,12 @@
 
         def finish(pair, carry):
             pieces = (2 * pair, 2 * pair + 1)
-            passed_in(phase, FILTERED, pair)
             both = strip_in.at[phase, FILTERED, pieces[0] : pieces[1] + 1]
             wait_for(both, strip_recv.at[phase, CHUNKS + pair])
-            filtered = [filter_cols(phase, FILTERED, q, f_ref[q]) for q in pieces]
-            for q, of_one_side in zip(pieces, filtered):
+            for q in pieces:
+                t_ref[q] = filter_cols(phase, FILTERED, q, f_ref[q])
+            passed_in(phase, FILTERED, pair)
+            for q in pieces:
                 rest = from_side(
                     phase,
                     FILTERED,
@@ -458,25 +465,29 @@
                         ((1, -1), [beside_in[phase, q, r].astype(F32) for r in range(2)]),
                     ),
                 )
-                t_ref[q] = of_one_side + rest
+                t_ref[q] = t_ref[q] + rest
             return member_sum(pieces, carry)
 
+        last = PAIRS - 1
         filter_own(0, 1)
         if phase == 0:
-            pass_on(phase, SOURCE, 0)
-            filter_own(2)
-            filter_one_side(0)
-            filter_own(3)
+            for pair in range(last):
+                pass_on(phase, SOURCE, pair)
+                filter_own(2 * pair + 2)
+                filter_one_side(pair)
+                filter_own(2 * pair + 3)
         else:
-            filter_own(2, 3)
-            pass_on(phase, SOURCE, 0)
+            filter_own(*range(2, CHUNKS))
+            for pair in range(last):
+                pass_on(phase, SOURCE, pair)
         come_beside(phase)
         before_last()
-        pass_on(phase, SOURCE, 1)
+        pass_on(phase, SOURCE, last)
         half_in()
         if phase == 1:
-            filter_one_side(0)
-        filter_one_side(1)
+            for pair in range(last):
+                filter_one_side(pair)
+        filter_one_side(last)
 
         carry = tuple(jnp.zeros((levels, cols), F32) for _ in range(2))
         if phase == 0:
@@ -486,9 +497,10 @@
         else:
             for pair in range(PAIRS):
                 pass_on(phase, FILTERED, pair)
-            carry = finish(0, carry)
-            near_end()
-            carry = finish(1, carry)
+            for pair in range(PAIRS):
+                if pair == PAIRS // 2:
+                    near_end()
+                carry = finish(pair, carry)
         for x in range(2):
             for h in range(2):
                 pmine[phase, h, x] = carry[x][h * half : (h + 1) * half]
@@ -584,11 +596,18 @@
         def _():
             wait_for(count_ref.at[0:n_z], red_send.at[which, 0])
 
+    state = {}
+
     def first_half_in():
+        innovation = target_value - gather(average[...])
         product = folded(noise * innovation * innovation) + dotted(0, None, range(CHUNKS))
         reduce_first(0, (folded(innovation * innovation), product))
-
-    grid_b = spread(0, scatter(innovation), lambda: None, first_half_in, lambda: None)
+        state["innovation"] = innovation
+
+    grid_b = spread(
+        0, values - counts * average[...], lambda: None, first_half_in, lambda: None
+    )
+    innovation = state["innovation"]
     gsum[ma] = gather(grid_b)
     g_copy = remote(gsum.at[ma], gsum.at[ma], g_sem.at[0], g_sem.at[1], partner)
     send_increment(0)
@@ -596,20 +615,18 @@
     g_copy.wait()
     image = gsum[0] + gsum[1] + noise * innovation
 
-    state = {}
-
     def before_last():
         norm_now, product = reduce_last(0)
         alpha = norm_now / product
         scaled = alpha * image
         residual = innovation - scaled
-        change = folded(scaled * (noise * scaled - 2.0 * image)) + dotted(1, alpha, (0, 1))
+        change = folded(scaled * (noise * scaled - 2.0 * image)) + dotted(1, alpha, range(CHUNKS - 2))
         state["step"] = norm_now, product, alpha, residual
         state["sums"] = folded(residual * residual), change
 
     def half_in():
         norm, change = state["sums"]
-        reduce_first(1, (norm, change + dotted(1, state["step"][2], (2, 3))))
+        reduce_first(1, (norm, change + dotted(1, state["step"][2], range(CHUNKS - 2, CHUNKS))))
 
     spread(1, scatter(image), before_last, half_in, lambda: reduce_second(1))
     send_increment(1)
@@ -664,6 +681,7 @@
             pltpu.VMEM((2, *shape), F32),
             pltpu.VMEM((2, 8, cols), F32),
             pltpu.VMEM((2, rows * levels, cols), F32),
+            pltpu.VMEM((rows * levels, cols), F32),
             pltpu.VMEM((rows, piece * 8, cols), F32),
             pltpu.VMEM((CHUNKS, rows * piece, cols), F32),
             pltpu.VMEM((CHUNKS, rows * piece, cols), F32),

time: 50.4 us -> 50.2 us (level)
  no operation moved by 1% of the time
where the time goes in v6:
time: 50.2 us; the launch traced here: 50.1 us
  Pallas kernels  48.3 us (96%)
  local copies, waits for them, and re-layouts  1.17 us (2%)
  between operations  0.64 us (1%)
    pallas_call x1, Pallas kernels, shards(): pl.pallas_call(functools.partial(kernel, n_gx, n_gy), out_shape=(pltpu.VM...  48.3 us
    unnamed x2, local copies, waits for them, and re-layouts  1.17 us

profile of v6, /device:TPU:1, one launch (start us, length us, event | category | flops | bytes accessed | tf_op | source)
XLA Modules:
  0.0 50.1 jit_solution(9074596473776420239)
XLA Ops:
  0.6 48.3 %analysis.1 = (f32[2,16,128]{2,1,0:T(8,128)S(1)}, f32[2,128]{1,0:T(2,128)S(1)}) custom-call(bf16[256,2,32,128]{3,2,1,0:T(8,128)(2,1)} %archive_hbm.1, s32[2,128]{1,0:T(2,128)} %bitcast.5, f32[2,128]{1,0:T(2,128)} %bitcast.6, f32[2,128]{1,0:T(2,128)} %bitcast.7), custom_call_target="tpu_custom_call" | custom-call | tf_op jit(solution)/shard_map/analysis/pallas_call | solution.py:670
  48.9 0.6 %copy.8 = f32[2,16,128]{2,1,0:T(8,128)} copy(f32[2,16,128]{2,1,0:T(8,128)S(1)} %get-tuple-element.6) | data formatting | bytes 32768
  49.5 0.6 %copy.9 = f32[256]{0:T(256)} copy(f32[256]{0:T(256)S(1)} %bitcast.4) | data formatting | bytes 2048

commit v7 on v6

--- a/solution.py
+++ b/solution.py
@@ -165,12 +165,10 @@
     def far_first(count):
         return sorted(range(1, count), key=lambda k: -min(k, count - k))
 
-    for k in far_first(n_gx):
-        pl.semaphore_signal(barrier, inc=1, device_id=row_block(k), device_id_type=MESH)
-    for k in far_first(n_plane):
-        across = {**plane_device(k), **row_block(1 - 2 * core)}
-        for device in (plane_device(k), across):
-            pl.semaphore_signal(barrier, inc=1, device_id=device, device_id_type=MESH)
+    greeted = [row_block(k) for k in far_first(n_gx) if min(k, n_gx - k) <= 4]
+    greeted += [col_block(k) for k in (2, -2, 1, -1)] + [{"ma": other}]
+    for device in greeted:
+        pl.semaphore_signal(barrier, inc=1, device_id=device, device_id_type=MESH)
 
     total = tuple(jnp.zeros((levels, cols), F32) for _ in range(2))
     for k in range(LOADS):
@@ -189,7 +187,7 @@
     meta[ma, 4:6, :] = pair_ref[1]
     meta[ma, 6:8, :] = jnp.zeros((2, cols), F32)
 
-    pl.semaphore_wait(barrier, n_gx - 1 + 2 * (n_plane - 1))
+    pl.semaphore_wait(barrier, len(greeted))
 
     partner = {"ma": other}
     meta_copy = remote(meta.at[ma], meta.at[ma], meta_sem.at[0], meta_sem.at[1], partner)
@@ -611,8 +609,8 @@
     gsum[ma] = gather(grid_b)
     g_copy = remote(gsum.at[ma], gsum.at[ma], g_sem.at[0], g_sem.at[1], partner)
     send_increment(0)
+    g_copy.wait()
     reduce_second(0)
-    g_copy.wait()
     image = gsum[0] + gsum[1] + noise * innovation
 
     def before_last():

time: 50.2 us -> 49.7 us (0.990)
  no operation moved by 1% of the time
where the time goes in v7:
time: 49.7 us
  Pallas kernels  47.8 us (96%)
  local copies, waits for them, and re-layouts  1.17 us (2%)
  between operations  0.64 us (1%)
    pallas_call x1, Pallas kernels, shards(): pl.pallas_call(functools.partial(kernel, n_gx, n_gy), out_shape=(pltpu.VM...  47.8 us
    unnamed x2, local copies, waits for them, and re-layouts  1.17 us

profile of v7, /device:TPU:1, one launch (start us, length us, event | category | flops | bytes accessed | tf_op | source)
XLA Modules:
  0.0 49.7 jit_solution(1823866010136934567)
XLA Ops:
  0.6 47.8 %analysis.1 = (f32[2,16,128]{2,1,0:T(8,128)S(1)}, f32[2,128]{1,0:T(2,128)S(1)}) custom-call(bf16[256,2,32,128]{3,2,1,0:T(8,128)(2,1)} %archive_hbm.1, s32[2,128]{1,0:T(2,128)} %bitcast.5, f32[2,128]{1,0:T(2,128)} %bitcast.6, f32[2,128]{1,0:T(2,128)} %bitcast.7), custom_call_target="tpu_custom_call" | custom-call | tf_op jit(solution)/shard_map/analysis/pallas_call | solution.py:668
  48.5 0.6 %copy.8 = f32[2,16,128]{2,1,0:T(8,128)} copy(f32[2,16,128]{2,1,0:T(8,128)S(1)} %get-tuple-element.6) | data formatting | bytes 32768
  49.1 0.6 %copy.9 = f32[256]{0:T(256)} copy(f32[256]{0:T(256)S(1)} %bitcast.4) | data formatting | bytes 2048

commit v8 on v7

--- a/solution.py
+++ b/solution.py
@@ -166,7 +166,8 @@
         return sorted(range(1, count), key=lambda k: -min(k, count - k))
 
     greeted = [row_block(k) for k in far_first(n_gx) if min(k, n_gx - k) <= 4]
-    greeted += [col_block(k) for k in (2, -2, 1, -1)] + [{"ma": other}]
+    for k in far_first(n_plane):
+        greeted += [plane_device(k), {**plane_device(k), **row_block(1 - 2 * core)}]
     for device in greeted:
         pl.semaphore_signal(barrier, inc=1, device_id=device, device_id_type=MESH)
 
@@ -491,6 +492,8 @@
         if phase == 0:
             for pair in range(PAIRS):
                 pass_on(phase, FILTERED, pair)
+                if pair == last:
+                    near_end()
                 carry = finish(pair, carry)
         else:
             for pair in range(PAIRS):
@@ -504,7 +507,7 @@
                 pmine[phase, h, x] = carry[x][h * half : (h + 1) * half]
         return jnp.concatenate(carry, axis=0)
 
-    def dotted(phase, factor, pieces):
+    def dotted(phase, pieces):
         total = None
         for q in pieces:
             way = course(SOURCE, q)
@@ -525,12 +528,7 @@
             field = halves(h_ref[phase, q])
             for i in range(2):
                 beside = beside_in[phase, q, i].astype(F32)
-                if factor is None:
-                    term = mine[i] * field[i] + theirs[i] * beside
-                else:
-                    term = (mine[i] * factor) * (field[i] * factor) + (theirs[i] * factor) * (
-                        beside * factor
-                    )
+                term = mine[i] * field[i] + theirs[i] * beside
                 total = term if total is None else total + term
         return jnp.sum(total, axis=0, keepdims=True)
 
@@ -598,35 +596,32 @@
 
     def first_half_in():
         innovation = target_value - gather(average[...])
-        product = folded(noise * innovation * innovation) + dotted(0, None, range(CHUNKS))
+        product = folded(noise * innovation * innovation) + dotted(0, range(CHUNKS))
         reduce_first(0, (folded(innovation * innovation), product))
         state["innovation"] = innovation
 
     grid_b = spread(
-        0, values - counts * average[...], lambda: None, first_half_in, lambda: None
+        0, values - counts * average[...], lambda: None, first_half_in, lambda: reduce_second(0)
     )
     innovation = state["innovation"]
     gsum[ma] = gather(grid_b)
     g_copy = remote(gsum.at[ma], gsum.at[ma], g_sem.at[0], g_sem.at[1], partner)
     send_increment(0)
     g_copy.wait()
-    reduce_second(0)
     image = gsum[0] + gsum[1] + noise * innovation
+    norm_now, product = reduce_last(0)
+    alpha = norm_now / product
+    residual = innovation - alpha * image
 
     def before_last():
-        norm_now, product = reduce_last(0)
-        alpha = norm_now / product
-        scaled = alpha * image
-        residual = innovation - scaled
-        change = folded(scaled * (noise * scaled - 2.0 * image)) + dotted(1, alpha, range(CHUNKS - 2))
-        state["step"] = norm_now, product, alpha, residual
-        state["sums"] = folded(residual * residual), change
+        product = folded(noise * residual * residual) + dotted(1, range(CHUNKS - 2))
+        state["sums"] = folded(residual * residual), product
 
     def half_in():
-        norm, change = state["sums"]
-        reduce_first(1, (norm, change + dotted(1, state["step"][2], range(CHUNKS - 2, CHUNKS))))
-
-    spread(1, scatter(image), before_last, half_in, lambda: reduce_second(1))
+        norm, product = state["sums"]
+        reduce_first(1, (norm, product + dotted(1, range(CHUNKS - 2, CHUNKS))))
+
+    spread(1, scatter(residual), before_last, half_in, lambda: reduce_second(1))
     send_increment(1)
     for phase in range(2):
         wait_for(sent_rows, block_send.at[phase])
@@ -634,9 +629,7 @@
     reduce_sent(0)
     wait_for(ptheirs.at[0], p_sem.at[0])
 
-    norm_now, product, alpha, residual = state["step"]
-    norm_next, change = reduce_last(1)
-    product = product + change
+    norm_next, product = reduce_last(1)
     ratio = norm_next / norm_now
     alpha_next = norm_next / (product - ratio * norm_next / alpha)
     weights = alpha * innovation + alpha_next * (residual + ratio * innovation)
@@ -645,9 +638,9 @@
     w_ref[1:2, :] = chosen[:, cols:]
 
     wait_for(ptheirs.at[1], p_sem.at[1])
-    first_weight = (alpha + alpha_next * (1.0 + ratio))[None]
-    second_weight = (alpha * alpha_next)[None]
-    inc_ref[...] = first_weight * (pmine[0, ma] + ptheirs[0]) - second_weight * (
+    first_weight = (alpha + alpha_next * ratio)[None]
+    second_weight = alpha_next[None]
+    inc_ref[...] = first_weight * (pmine[0, ma] + ptheirs[0]) + second_weight * (
         pmine[1, ma] + ptheirs[1]
     )
 

time: 49.7 us -> 50.2 us (1.010)
  no operation moved by 1% of the time
where the time goes in v8:
time: 50.2 us; the launch traced here: 50.1 us
  Pallas kernels  48.3 us (96%)
  local copies, waits for them, and re-layouts  1.17 us (2%)
  between operations  0.64 us (1%)
    pallas_call x1, Pallas kernels, shards(): pl.pallas_call(functools.partial(kernel, n_gx, n_gy), out_shape=(pltpu.VM...  48.3 us
    unnamed x2, local copies, waits for them, and re-layouts  1.17 us

profile of v8, /device:TPU:1, one launch (start us, length us, event | category | flops | bytes accessed | tf_op | source)
XLA Modules:
  0.0 50.1 jit_solution(8169585760394184795)
XLA Ops:
  0.6 48.3 %analysis.1 = (f32[2,16,128]{2,1,0:T(8,128)S(1)}, f32[2,128]{1,0:T(2,128)S(1)}) custom-call(bf16[256,2,32,128]{3,2,1,0:T(8,128)(2,1)} %archive_hbm.1, s32[2,128]{1,0:T(2,128)} %bitcast.5, f32[2,128]{1,0:T(2,128)} %bitcast.6, f32[2,128]{1,0:T(2,128)} %bitcast.7), custom_call_target="tpu_custom_call" | custom-call | tf_op jit(solution)/shard_map/analysis/pallas_call | solution.py:661
  48.9 0.6 %copy.8 = f32[2,16,128]{2,1,0:T(8,128)} copy(f32[2,16,128]{2,1,0:T(8,128)S(1)} %get-tuple-element.6) | data formatting | bytes 32768
  49.6 0.6 %copy.9 = f32[256]{0:T(256)} copy(f32[256]{0:T(256)S(1)} %bitcast.4) | data formatting | bytes 2048
